TPU v7x, 128 devices: a whole 4x4x4 slice. The times are simulated.
128 devices in a mesh: gx: 2 (over core), gy: 4 (over x), gz: 16 (over z, y).
Axes of the slice: x: 4, y: 4, z: 4, core: 2. Of those that a mesh axis runs over, the one named last changes fastest.
Arguments:
- permanent_field: float32 [12, 24, 96, 3], P('gx', 'gy', 'gz'), may hold values from -6 to 6
- polar: float32 [12, 24, 96], P('gx', 'gy', 'gz'), may hold values from 0.4 to 1.4
- jitter: float32 [12, 24, 96, 3], P('gx', 'gy', 'gz'), may hold values from -0.2 to 0.2
- neighbors: int32 [12, 24, 96, 56], P('gx', 'gy', 'gz'), may hold values from -1 to 987, as said below
Outputs:
- dipoles: float32 [12, 24, 96, 3], P('gx', 'gy', 'gz')
- residual: float32 [12, 24, 96, 3], P('gx', 'gy', 'gz')
- step_lengths: float32 [8], replicated
Inputs may be any that keep to these rules, and one draw needn't show every extreme that they name: `neighbors`: each entry is -1 or the flat index of a neighbour in the device's block extended by two sites on every side, with an offset d of squared length 1 to 5 (each component -2 to 2), each offset at most once in a row; the -1 entries come after all others; if site j stands in site i's row with offset d then i stands in j's row with offset -d, the box being periodic.
All inputs are finite; a program needn't handle non-finite values.
Results may differ from a plain program's by a relative error of at most 0.0003.
Values sent between devices are 32-bit elements.
A program may use at most 64 MiB of HBM per device.

v0:
```python
import functools

import jax
import jax.numpy as jnp
from jax import lax
from jax.experimental import pallas as pl
from jax.experimental.pallas import tpu as pltpu
from jax.sharding import PartitionSpec as P

ITERS = 8
MESH = pl.DeviceIdType.MESH
thole_damping = 0.39
site_spacing = 3.5
ROWS, LANES = 8, 128


def stencil():
    return [
        (a, b, c)
        for a in range(-2, 3)
        for b in range(-2, 3)
        for c in range(-2, 3)
        if 1 <= a * a + b * b + c * c <= 5
    ]


def roll(value, shift):
    shift = shift % LANES
    return value if shift == 0 else pltpu.roll(value, shift, axis=1)


def kernel(
    sizes, edge,
    nb_ref, in_ref, x_out, r_out, len_out,
    ext, w_ext, r_ext, s_ext, geo, coef, chip_src, chip_dst, core_src, core_dst, dot_src, dot_dst,
    halo_send, halo_recv, dot_send, dot_recv,
):
    nx, ny, nz = sizes
    wide = edge + 4
    offsets = stencil()
    gx, gy, gz = lax.axis_index("gx"), lax.axis_index("gy"), lax.axis_index("gz")
    rank = (gx * ny + gy) * nz + gz

    def at(ox, oy, oz):
        return (lax.rem(gx + ox + nx, nx), lax.rem(gy + oy + ny, ny), lax.rem(gz + oz + nz, nz))

    others = [
        (a, b, c) for a in range(nx) for b in range(ny) for c in range(nz) if (a, b, c) != (0, 0, 0)
    ]
    others.sort(key=lambda o: -(min(o[0], nx - o[0]) + 2 * min(o[1], ny - o[1]) + 2 * min(o[2], nz - o[2])))

    barrier = pltpu.get_barrier_semaphore()
    for o in others:
        pl.semaphore_signal(barrier, inc=1, device_id=at(*o), device_id_type=MESH)

    lane = lax.broadcasted_iota(jnp.int32, (ROWS, LANES), 1)
    row = lax.broadcasted_iota(jnp.int32, (ROWS, LANES), 0)
    ye = lane // wide
    ze = lane - ye * wide
    y_low, y_high = ye < 2, (ye >= edge + 2) & (ye < wide)
    y_mid = (ye >= 2) & (ye < edge + 2)
    z_low, z_high = ze < 2, ze >= edge + 2
    z_mid = (ze >= 2) & (ze < edge + 2)
    src_zp = (ze >= edge) & z_mid
    src_zm = (ze < 4) & z_mid
    src_yp = (ye >= edge) & y_mid
    src_ym = (ye < 4) & y_mid

    def pack(planes, mask, base, step):
        out = None
        for c, plane in enumerate(planes):
            part = roll(jnp.where(mask, plane, 0.0), base + c * step)
            out = part if out is None else out + part
        return out

    def halo_copies(par, groups, comps):
        copies = []
        for oy in (-1, 1, 0):
            for oz in (-1, 1, 0):
                for ox in (1, 0):
                    if (ox, oy, oz) == (0, 0, 0):
                        continue
                    back = ox * 9 + (1 - oy) * 3 + 1 - oz
                    here = ox * 9 + (1 + oy) * 3 + 1 + oz
                    if oy == 0 and oz == 0:
                        src, dst = core_src.at[par, pl.ds(0, comps)], core_dst.at[par, pl.ds(0, comps)]
                    else:
                        kind = {1: 0, -1: 1}[oz] if oz else {1: 2, -1: 3}[oy]
                        src = chip_src.at[par, kind, pl.ds(0, groups)]
                        dst = chip_dst.at[par, back, pl.ds(0, groups)]
                    copies.append(
                        pltpu.make_async_remote_copy(
                            src_ref=src, dst_ref=dst,
                            send_sem=halo_send.at[par, here], recv_sem=halo_recv.at[par, back],
                            device_id=at(ox, oy, oz), device_id_type=MESH,
                        )
                    )
        return copies

    def halo_start(par, planes):
        parts = [planes] if len(planes) <= 4 else [planes[:4], planes[4:]]
        for g, part in enumerate(parts):
            chip_src[par, 0, g] = pack(part, src_zp, -edge, 2)
            chip_src[par, 1, g] = pack(part, src_zm, edge, -2)
            chip_src[par, 2, g] = pack(part, src_yp, -edge * wide, 2 * wide)
            chip_src[par, 3, g] = pack(part, src_ym, edge * wide, -2 * wide)
        for c, plane in enumerate(planes):
            core_src[par, c] = plane
        copies = halo_copies(par, len(parts), len(planes))
        for copy in copies:
            copy.start()
        return copies

    def halo_finish(par, planes, copies, target):
        for copy in copies:
            copy.wait_recv()
        parts = [planes] if len(planes) <= 4 else [planes[:4], planes[4:]]
        index = 0
        for g, part in enumerate(parts):
            merged = []
            for ox in (0, 1):
                def got(oy, oz):
                    return chip_dst[par, ox * 9 + (1 + oy) * 3 + 1 + oz, g]

                def column(oz):
                    near = got(0, oz)
                    low = roll(got(-1, oz), -edge * wide)
                    high = roll(got(1, oz), edge * wide)
                    return jnp.where(y_mid, near, jnp.where(y_low, low, high))

                merged.append((column(-1), column(1), got(-1, 0), got(1, 0)))
            for c, plane in enumerate(part):
                full = []
                for ox in (0, 1):
                    zl, zh, yl, yh = merged[ox]
                    base = plane if ox == 0 else core_dst[par, index]
                    base = jnp.where(y_low & z_mid, roll(yl, -2 * wide * c), base)
                    base = jnp.where(y_high & z_mid, roll(yh, 2 * wide * c), base)
                    base = jnp.where(z_low, roll(zl, -2 * c), base)
                    base = jnp.where(z_high, roll(zh, 2 * c), base)
                    full.append(jnp.where(ye < wide, base, 0.0))
                ref, k = target[index]
                ref[k, pl.ds(2, edge), :] = full[0][:edge]
                ref[k, pl.ds(0, 2), :] = full[1][edge - 2 : edge]
                ref[k, pl.ds(edge + 2, 2), :] = full[1][0:2]
                index += 1
        for copy in copies:
            copy.wait_send()

    inputs = [in_ref[c] for c in range(7)]
    live = (row < edge) & y_mid & z_mid & (ye < wide)
    jit, pol, field = inputs[0:3], jnp.where(live, inputs[3], 1.0), inputs[4:7]
    inv = 1.0 / pol
    x = [pol * f for f in field]
    ext[...] = jnp.zeros_like(ext)
    geo[...] = jnp.ones_like(geo)
    for ref in (w_ext, r_ext, s_ext):
        ref[...] = jnp.zeros_like(ref)

    pl.semaphore_wait(barrier, len(others))
    first = [*jit, pol, *x]
    copies = halo_start(0, first)

    home = row * (wide * wide) + lane + 2 * wide * wide
    hundred, ten = wide * wide, wide

    def slot(number, words):
        entry = nb_ref[number]
        rel = entry - home + (2 * hundred + hundred // 2)
        dx = (rel * 5243) >> 19
        rem = rel - dx * hundred - (hundred // 2 - 2 * ten - 5)
        dy = (rem * 6554) >> 16
        dz = rem - dy * ten - 3
        bit = jnp.where(entry >= 0, jnp.left_shift(1, jnp.clip(dy * 5 + dz, 0, 24)), 0)
        return tuple(word | jnp.where(dx == k, bit, 0) for k, word in enumerate(words))

    zero = jnp.zeros((ROWS, LANES), jnp.int32)
    words = lax.fori_loop(0, nb_ref.shape[0], slot, (zero,) * 5)

    halo_finish(0, first, copies, [(geo, 0), (geo, 1), (geo, 2), (geo, 3), (ext, 0), (ext, 1), (ext, 2)])

    for n, d in enumerate(offsets):
        shift = -(d[1] * wide + d[2])
        bit = 5 * (d[1] + 2) + d[2] + 2
        present = (words[d[0] + 2] & (1 << bit)) != 0
        near = [roll(geo[k, pl.ds(d[0] + 2, ROWS), :], shift) for k in range(4)]
        sep = [
            jnp.where(present, (d[k] + near[k] - jit[k]) * site_spacing, site_spacing) for k in range(3)
        ]
        sq = sep[0] * sep[0] + sep[1] * sep[1] + sep[2] * sep[2]
        dist = jnp.sqrt(sq)
        cube = sq * dist
        damp = thole_damping * cube / jnp.sqrt(pol * near[3])
        fall = jnp.exp(-damp)
        iso = jnp.where(present, (1.0 - fall) / cube, 0.0)
        rad = jnp.where(present, 3.0 * (1.0 - (1.0 + damp) * fall) / (cube * sq), 0.0)
        rs = [rad * s for s in sep]
        coef[n, 0] = rs[0] * sep[0] - iso
        coef[n, 1] = rs[0] * sep[1]
        coef[n, 2] = rs[0] * sep[2]
        coef[n, 3] = rs[1] * sep[1] - iso
        coef[n, 4] = rs[1] * sep[2]
        coef[n, 5] = rs[2] * sep[2] - iso

    def operate(planes):
        acc = [[None] * 5 for _ in range(3)]
        for n, d in enumerate(offsets):
            shift = -(d[1] * wide + d[2])
            a, b, c = [roll(ext[k, pl.ds(d[0] + 2, ROWS), :], shift) for k in range(3)]
            xx, xy, xz, yy, yz, zz = [coef[n, k] for k in range(6)]
            for k, term in enumerate(
                (xx * a + xy * b + xz * c, xy * a + yy * b + yz * c, xz * a + yz * b + zz * c)
            ):
                old = acc[k][d[0] + 2]
                acc[k][d[0] + 2] = term if old is None else old + term
        return [
            planes[k] * inv - (((acc[k][0] + acc[k][1]) + (acc[k][3] + acc[k][4])) + acc[k][2])
            for k in range(3)
        ]

    image = operate(x)
    r = [jnp.where(live, field[k] - image[k], 0.0) for k in range(3)]
    u = [pol * v for v in r]
    copies = halo_start(1, r)
    halo_finish(1, r, copies, [(r_ext, 0), (r_ext, 1), (r_ext, 2)])
    for k in range(3):
        ext[k] = geo[3] * r_ext[k]
    w = operate(u)

    pick = lax.broadcasted_iota(jnp.int32, (1, LANES), 1)

    def dot_copies(par):
        return [
            pltpu.make_async_remote_copy(
                src_ref=dot_src.at[par], dst_ref=dot_dst.at[par, rank],
                send_sem=dot_send.at[par, k], recv_sem=dot_recv.at[par, k],
                device_id=at(*o), device_id_type=MESH,
            )
            for k, o in enumerate(others)
        ]

    def total(value):
        return jnp.sum(jnp.sum(value, axis=0, keepdims=True), axis=1, keepdims=True)

    def dots_start(par, r, u, w):
        gamma = total(r[0] * u[0] + r[1] * u[1] + r[2] * u[2])
        delta = total(w[0] * u[0] + w[1] * u[1] + w[2] * u[2])
        line = jnp.where(pick == 0, gamma, jnp.where(pick == 1, delta, 0.0))
        dot_src[par] = line
        dot_dst[par, rank] = line
        copies = dot_copies(par)
        for copy in copies:
            copy.start()
        return copies

    def dots_finish(par, copies):
        for copy in copies:
            copy.wait_recv()
        line = jnp.sum(dot_dst[par, :, 0, :], axis=0, keepdims=True)
        for copy in copies:
            copy.wait_send()
        gamma = jnp.sum(jnp.where(pick == 0, line, 0.0), axis=1, keepdims=True)
        delta = jnp.sum(jnp.where(pick == 1, line, 0.0), axis=1, keepdims=True)
        return gamma, delta

    def lengths(number, gamma, delta, gamma_old, step_old):
        beta = gamma / gamma_old
        step = gamma / (delta - beta * gamma / step_old)
        len_out[pl.ds(number, 1), :] = jnp.broadcast_to(step, (1, LANES))
        return beta, step

    def axpy(a, s, b):
        return [a[k] + s * b[k] for k in range(3)]

    def iteration(number, state):
        x, r, u, w, p, s, gamma_old, step_old = state
        par = lax.rem(number, 2)
        dots = dots_start(par, r, u, w)
        halos = halo_start(par, w)
        halo_finish(par, w, halos, [(w_ext, 0), (w_ext, 1), (w_ext, 2)])
        gamma, delta = dots_finish(par, dots)
        beta, step = lengths(number, gamma, delta, gamma_old, step_old)
        for k in range(3):
            s_new = w_ext[k] + beta * s_ext[k]
            r_new = r_ext[k] - step * s_new
            s_ext[k] = s_new
            r_ext[k] = r_new
            ext[k] = geo[3] * r_new
        s, p = axpy(w, beta, s), axpy(u, beta, p)
        x, r = axpy(x, step, p), axpy(r, -step, s)
        u = [pol * v for v in r]
        w = operate(u)
        return x, r, u, w, p, s, gamma, step

    none = [jnp.zeros((ROWS, LANES), jnp.float32)] * 3
    far = jnp.full((1, 1), jnp.inf, jnp.float32)
    one = jnp.ones((1, 1), jnp.float32)
    state = (x, r, u, w, none, none, far, one)
    x, r, u, w, p, s, gamma_old, step_old = lax.fori_loop(0, ITERS - 1, iteration, state)
    last = (ITERS - 1) % 2
    dots = dots_start(last, r, u, w)
    gamma, delta = dots_finish(last, dots)
    beta, step = lengths(ITERS - 1, gamma, delta, gamma_old, step_old)
    p, s = axpy(u, beta, p), axpy(w, beta, s)
    x, r = axpy(x, step, p), axpy(r, -step, s)
    for k in range(3):
        x_out[k] = x[k]
        r_out[k] = r[k]


def solution(mesh):
    sizes = tuple(mesh.shape[a] for a in ("gx", "gy", "gz"))
    assert sizes[0] == 2
    count = sizes[0] * sizes[1] * sizes[2]

    def local(permanent_field, polar, jitter, neighbors):
        edge = polar.shape[0]
        wide = edge + 4
        slots = neighbors.shape[-1]

        def spread(array, fill):
            array = jnp.moveaxis(array, -1, 0)
            array = jnp.pad(array, ((0, 0), (0, ROWS - edge), (2, 2), (2, 2)), constant_values=fill)
            array = array.reshape(array.shape[0], ROWS, wide * wide)
            return jnp.pad(array, ((0, 0), (0, 0), (0, LANES - wide * wide)), constant_values=fill)

        bundle = jnp.concatenate([jitter, polar[..., None], permanent_field], axis=-1)
        bundle = spread(bundle, 0.0)
        plane = jax.ShapeDtypeStruct((3, ROWS, LANES), jnp.float32)
        vmem = pl.BlockSpec(memory_space=pltpu.VMEM)
        f32 = jnp.float32
        x, r, steps = pl.pallas_call(
            functools.partial(kernel, sizes, edge),
            out_shape=(plane, plane, jax.ShapeDtypeStruct((ITERS, LANES), f32)),
            in_specs=[vmem, vmem],
            out_specs=(vmem, vmem, vmem),
            scratch_shapes=[
                *[pltpu.VMEM((3, 16, LANES), f32)] * 4,
                pltpu.VMEM((4, 16, LANES), f32),
                pltpu.VMEM((len(stencil()), 6, ROWS, LANES), f32),
                pltpu.VMEM((2, 4, 2, ROWS, LANES), f32),
                pltpu.VMEM((2, 18, 2, ROWS, LANES), f32),
                pltpu.VMEM((2, 7, ROWS, LANES), f32),
                pltpu.VMEM((2, 7, ROWS, LANES), f32),
                pltpu.VMEM((2, 1, LANES), f32),
                pltpu.VMEM((2, count, 1, LANES), f32),
                pltpu.SemaphoreType.DMA((2, 18)),
                pltpu.SemaphoreType.DMA((2, 18)),
                pltpu.SemaphoreType.DMA((2, count)),
                pltpu.SemaphoreType.DMA((2, count)),
            ],
            compiler_params=pltpu.CompilerParams(collective_id=0, has_side_effects=True),
        )(spread(neighbors, -1), bundle)

        def gather(planes):
            planes = planes[:, :edge, : wide * wide].reshape(3, edge, wide, wide)
            return jnp.moveaxis(planes[:, :, 2:-2, 2:-2], 0, -1)

        return gather(x), gather(r), steps[:, 0]

    return jax.shard_map(
        local,
        mesh=mesh,
        in_specs=(
            P("gx", "gy", "gz", None),
            P("gx", "gy", "gz"),
            P("gx", "gy", "gz", None),
            P("gx", "gy", "gz", None),
        ),
        out_specs=(P("gx", "gy", "gz", None), P("gx", "gy", "gz", None), P()),
        check_vma=False,
    )
```

profile of v0, /device:TPU:1, one launch (start us, length us, event | category | flops | bytes accessed | tf_op | source)
XLA Modules:
  0.0 98.6 jit_solution(15706594324809269057)
XLA Ops:
  0.6 0.8 copy.13
  1.4 1.0 %maximum_bitcast_fusion = f32[7,6,6,6]{3,0,2,1:T(8,128)S(1)} fusion(f32[6,6,6,3]{2,3,1,0:T(4,128)} %param.4, f32[6,6,6,1]{2,3,1,0:T(1,128)S(1)} %copy.13, f32[6,6,6,3]{2,3,1,0:T(4,128)} %param.6), kind=kLoop, calls=%fused_computation | loop fusion | flops 3024 | bytes 12096 | tf_op jit(solution)/shard_map/transpose | solution.py:322
  2.4 0.0 copy-start
  2.4 0.9 copy-done
  3.4 0.2 copy.12
  3.6 0.7 pad.17.nb_ref
  4.3 0.2 pad.18.clone
  4.5 0.2 reshape.19
  4.6 0.6 pad.19.in_ref
  5.2 90.2 %shard_map.67 = (f32[3,8,128]{2,1,0:T(8,128)}, f32[3,8,128]{2,1,0:T(8,128)}, f32[8,128]{1,0:T(8,128)}) custom-call(s32[56,8,128]{2,1,0:T(8,128)} %pad.17.nb_ref, f32[7,8,128]{2,1,0:T(8,128)} %pad.19.in_ref), custom_call_target="tpu_custom_call" | custom-call | tf_op jit(solution)/shard_map/pallas_call | solution.py:332
  95.5 0.0 copy-start.2
  95.5 1.3 %slice_reduce_fusion = f32[8]{0:T(128)} fusion(f32[8,128]{1,0:T(8,128)} %get-tuple-element.8), kind=kLoop, calls=%fused_computation.3 | loop fusion | bytes 64 | tf_op jit(solution)/shard_map/slice | solution.py:359
  96.8 0.0 copy-done.2
  96.8 0.1 reshape.21
  96.9 0.1 slice_bitcast_fusion
  97.0 0.0 copy-start.1
  97.0 0.7 copy.16
  97.7 0.0 copy-done.1
  97.7 0.1 reshape.20
  97.8 0.1 slice_bitcast_fusion.1
  97.9 0.7 copy.15
  (3 shorter events, 0.1 us)
Async XLA Ops:
  2.4 0.9 copy-start
  95.5 1.3 %copy-start.2 = (f32[3,8,128]{2,1,0:T(8,128)S(1)}, f32[3,8,128]{2,1,0:T(8,128)}, u32[]{:S(2)}) copy-start(f32[3,8,128]{2,1,0:T(8,128)} %get-tuple-element.7) | copy-start | bytes 36868
  97.0 0.7 copy-start.1
where the time goes:
time: 98.9 us; the launch traced here: 98.6 us
  Pallas kernels  90.2 us (91%)
  local copies, waits for them, and re-layouts  6.6 us (7%)
  other arithmetic  0.99 us (1%)
    pallas_call x1, Pallas kernels, local(): pl.pallas_call(functools.partial(kernel, sizes, edge), out_shape=(plane,...  90.2 us
    unnamed x10, local copies, waits for them, and re-layouts  2.3 us

commit v1 on v0

v1 whole, which is shorter than its diff:
```python
import functools

import jax
import jax.numpy as jnp
from jax import lax
from jax.experimental import pallas as pl
from jax.experimental.pallas import tpu as pltpu
from jax.sharding import PartitionSpec as P

ITERS = 8
BLOCKS = (2, 3, 3)
MESH = pl.DeviceIdType.MESH
thole_damping = 0.39
site_spacing = 3.5
ROWS, LANES = 8, 128
EDGE = 6
WIDE = 3 * EDGE
ORIGIN = 2 * WIDE + 2
OWN = EDGE * WIDE + EDGE - ORIGIN
f32 = jnp.float32

STENCIL = [
    (a, b, c)
    for a in range(-2, 3)
    for b in range(-2, 3)
    for c in range(-2, 3)
    if 1 <= a * a + b * b + c * c <= 5
]
SHIFTS = sorted({(b, c) for a, b, c in STENCIL})
SPAN = [[d[0] for d in STENCIL if d[1:] == s] for s in SHIFTS]
FIRST = [sum(len(v) for v in SPAN[:i]) for i in range(len(SHIFTS))]
HOME = SHIFTS.index((0, 0))
FORWARD = [d for d in STENCIL if d > (0, 0, 0)]


def flag_places():
    room = {0: 9, 1: 10, 2: 10}
    used = {0: 0, 1: 0, 2: 0}
    places = {}
    for d in FORWARD:
        c = d[0] if used[d[0]] < room[d[0]] else 2
        if d[0] != 2 and used[d[0]] >= room[d[0]]:
            c = 2
        places[d] = (c, used[c])
        used[c] += 1
    assert used[2] <= room[2]
    return places


FLAGS = flag_places()
FLAG_TILES = 9
TILES = 3 + FLAG_TILES


def roll(value, shift):
    shift = shift % LANES
    return value if shift == 0 else pltpu.roll(value, shift, axis=1)


def kernel(
    sizes,
    field_ref, pol_ref, jit_ref, nb_ref, x_out, r_out, len_out,
    ext, sh, geo, words, sgeo, sword, polo, coef, chain, state,
    send0, recv0, send1, recv1, dot_src, dot_dst,
    halo_send, halo_recv, dot_send, dot_recv,
):
    nx, ny, nz = sizes
    count = nx * ny * nz
    gx, gy, gz = lax.axis_index("gx"), lax.axis_index("gy"), lax.axis_index("gz")
    rank = (gx * ny + gy) * nz + gz

    def at(ox, oy, oz):
        return (lax.rem(gx + ox + nx, nx), lax.rem(gy + oy + ny, ny), lax.rem(gz + oz + nz, nz))

    others = [
        (a, b, c) for a in range(nx) for b in range(ny) for c in range(nz) if (a, b, c) != (0, 0, 0)
    ]
    others.sort(key=lambda o: -(min(o[0], nx - o[0]) + 2 * min(o[1], ny - o[1]) + 2 * min(o[2], nz - o[2])))

    barrier = pltpu.get_barrier_semaphore()
    for o in others:
        pl.semaphore_signal(barrier, inc=1, device_id=at(*o), device_id_type=MESH)

    lane = lax.broadcasted_iota(jnp.int32, (ROWS, LANES), 1)
    row = lax.broadcasted_iota(jnp.int32, (ROWS, LANES), 0)
    pick = lax.broadcasted_iota(jnp.int32, (1, LANES), 1)

    def third(b):
        position = lax.rem(lane - 108 * b + 2 * LANES * 2, LANES)
        within = position - (position // WIDE) * WIDE
        return within < EDGE, within < 2 * EDGE

    zone = [third(b) for b in range(3)]
    packed = (row < EDGE) & (lane < EDGE * WIDE)

    def gather3(ref, comps):
        out = jnp.zeros((ROWS, LANES), f32)
        for y in range(EDGE):
            for c in range(comps):
                part = ref[:, y, c, :] if comps == 3 else ref[:, y, :]
                part = jnp.concatenate([part, jnp.zeros((EDGE, LANES - EDGE), f32)], axis=1)
                part = jnp.concatenate([part, jnp.zeros((ROWS - EDGE, LANES), f32)], axis=0)
                out = out + roll(part, y * WIDE + c * EDGE)
        return out

    field, jit = gather3(field_ref, 3), gather3(jit_ref, 3) * site_spacing
    pol0 = gather3(pol_ref, 1)
    polp = pol0 + roll(pol0, EDGE) + roll(pol0, 2 * EDGE)
    weight = jnp.where(packed, 1.0 / jnp.where(packed, polp, 1.0), 0.0)
    x = polp * field

    slots = nb_ref.shape[3]
    plane = lax.broadcasted_iota(jnp.int32, (EDGE, slots), 0) * 100
    spread = [jnp.zeros((ROWS, LANES), f32) for _ in range(3)]
    for y in range(EDGE):
        for z in range(EDGE):
            entry = nb_ref[:, y, z, :]
            code = entry - plane - (222 + 10 * y + z)
            real = code > 0
            code = code + 22
            dx = jnp.where(code >= 200, 2, jnp.where(code >= 100, 1, 0))
            rem = code - dx * 100
            bit = rem - 5 * ((rem * 205) >> 11) - 2
            value = jnp.where(real, jnp.left_shift(1, jnp.where(real, bit, 0)), 0).astype(f32)
            for k in range(3):
                total = jnp.sum(jnp.where(dx == k, value, 0.0), axis=1, keepdims=True)
                total = jnp.concatenate([total, jnp.zeros((ROWS - EDGE, 1), f32)], axis=0)
                spread[k] = spread[k] + jnp.where(lane == y * WIDE + k * EDGE + z, total, 0.0)
    bits = [s.astype(jnp.int32) for s in spread]
    moved = {}

    def flag_tile(n):
        out = jnp.zeros((ROWS, LANES), jnp.int32)
        for d, (c, m) in FLAGS.items():
            if m == n:
                key = (d[0], c)
                if key not in moved:
                    moved[key] = roll(bits[d[0]], (c - d[0]) * EDGE)
                out = out | (lax.shift_right_logical(moved[key], 5 * (d[1] + 2) + d[2]) & 1)
        return out.astype(f32)

    send0[0] = jit
    send0[1] = x
    send0[2] = pol0 + flag_tile(FLAG_TILES)
    for n in range(FLAG_TILES):
        send0[3 + n] = flag_tile(n)
    own = 4
    recv0[own] = send0[...]

    def halo_start(index, src, dst):
        copies = []
        for oy in (-1, 1, 0):
            for oz in (-1, 1, 0):
                for ox in (1, 0):
                    if (ox, oy, oz) == (0, 0, 0):
                        continue
                    back = ox * 9 + (1 - oy) * 3 + 1 - oz
                    here = ox * 9 + (1 + oy) * 3 + 1 + oz
                    copies.append(
                        pltpu.make_async_remote_copy(
                            src_ref=src, dst_ref=dst.at[back],
                            send_sem=halo_send.at[index, here], recv_sem=halo_recv.at[index, back],
                            device_id=at(ox, oy, oz), device_id_type=MESH,
                        )
                    )
        for copy in copies:
            copy.start()
        return copies

    def assemble(get, c, target, fill=0.0):
        full = []
        for h in range(2):
            part = []
            for b in range(3):
                m = [roll(get(h * 9 + b * 3 + k), 108 * b + EDGE * (k - c)) for k in range(3)]
                part.append(jnp.where(zone[b][0], m[0], jnp.where(zone[b][1], m[1], m[2])))
            full.append((
                jnp.where(lane < 108, part[0], part[1]),
                jnp.where(lane < 88, part[1], part[2]),
                jnp.where(lane < 68, part[2], fill),
            ))
        for t in range(3):
            target[t, 2:8, :] = full[0][t][:6]
            target[t, 8:14, :] = full[1][t][:6]
            target[t, 0:2, :] = full[1][t][4:6]
            target[t, 14:16, :] = full[0][t][:2]

    def wide_shift(get, put):
        for half in range(2):
            rows = pl.ds(8 * half, 8)
            v = [get(t, rows) for t in range(3)]
            for i, (dy, dz) in enumerate(SHIFTS):
                a = ORIGIN + dy * WIDE + dz
                r = [roll(u, -a) for u in v]
                for t in range(2):
                    put(i, t, rows, jnp.where(lane < LANES - a, r[t], r[t + 1]))

    def near_shift(get, put):
        for half in range(2):
            rows = pl.ds(8 * half, 8)
            v = [get(t, rows) for t in range(2)]
            for i, (dy, dz) in enumerate(SHIFTS):
                s = dy * WIDE + dz
                r = [roll(u, -s) for u in v]
                if s > 0:
                    r[0] = jnp.where(lane < LANES - s, r[0], r[1])
                elif s < 0:
                    r[1] = jnp.where(lane >= -s, r[1], r[0])
                for t in range(2):
                    put(i, t, rows, r[t])

    def apply(source, target, last):
        def shift(k, carry):
            def put(i, t, rows, value):
                sh[i, t, k, rows, :] = value

            if source is None:
                wide_shift(lambda t, rows: ext[k, t, rows, :], put)
            else:
                near_shift(lambda t, rows: chain[source, k, t, rows, :], put)
            return carry

        lax.fori_loop(0, 3, shift, 0)

        def tile(t, carry):
            for rt in range(1 if last else 2):
                acc = [[None, None] for _ in range(3)]
                for i in range(len(SHIFTS)):
                    for j, dx in enumerate(SPAN[i]):
                        n = FIRST[i] + j
                        a, b, c = [sh[i, t, k, pl.ds(dx + 2 + 4 * rt, 8), :] for k in range(3)]
                        xx, xy, xz, yy, yz, zz = [coef[t, rt, n, k] for k in range(6)]
                        for k, term in enumerate((
                            xx * a + xy * b + xz * c, xy * a + yy * b + yz * c, xz * a + yz * b + zz * c,
                        )):
                            old = acc[k][n % 2]
                            acc[k][n % 2] = term if old is None else old + term
                scale = polo[t, pl.ds(2 + 4 * rt, 8), :]
                for k in range(3):
                    out = (acc[k][0] + acc[k][1]) * scale
                    chain[target, k, t, pl.ds(2 + 4 * rt, 8), :] = out
                    if not last:
                        if rt == 0:
                            chain[target, k, t, 14:16, :] = out[0:2]
                        else:
                            chain[target, k, t, 0:2, :] = out[6:8]
            return carry

        lax.fori_loop(0, 2, tile, 0)

    def pack(index):
        parts = []
        for k in range(3):
            a = OWN - EDGE * k
            r = [roll(chain[index, k, t, 2:10, :], -a) for t in range(2)]
            parts.append(jnp.where(lane < LANES - a, r[0], r[1]))
        out = jnp.where(zone[0][0], parts[0], jnp.where(zone[0][1], parts[1], parts[2]))
        return jnp.where(packed, out, 0.0)

    pl.semaphore_wait(barrier, len(others))
    copies0 = halo_start(0, send0, recv0)
    chain[...] = jnp.zeros_like(chain)
    for copy in copies0:
        copy.wait_recv()

    for k in range(3):
        assemble(lambda b: recv0[b, 0], k, geo.at[k])
        assemble(lambda b: recv0[b, 1], k, ext.at[k])
    assemble(lambda b: recv0[b, 2], 0, geo.at[4], 1.0)
    geo[3] = lax.rsqrt(geo[4])
    flagged = [
        jnp.where(zone[0][0], 0.0, recv0[b, 2]) * float(2 ** FLAG_TILES) for b in range(18)
    ]
    for n in range(FLAG_TILES):
        for b in range(18):
            flagged[b] = flagged[b] + recv0[b, 3 + n] * float(2 ** n)
    for b in range(18):
        state[0, b] = flagged[b]
    for k in range(3):
        assemble(lambda b: state[0, b], k, words.at[k])

    def shift_geo(k, carry):
        def put(i, t, rows, value):
            sgeo[i, t, k, rows, :] = value

        wide_shift(lambda t, rows: geo[k, t, rows, :], put)
        return carry

    lax.fori_loop(0, 4, shift_geo, 0)

    def shift_words(k, carry):
        def put(i, t, rows, value):
            sword[i, t, k, rows, :] = value.astype(jnp.int32)

        wide_shift(lambda t, rows: words[k, t, rows, :], put)
        return carry

    lax.fori_loop(0, 3, shift_words, 0)
    for half in range(2):
        rows = pl.ds(8 * half, 8)
        r = [roll(geo[4, t, rows, :], -ORIGIN) for t in range(3)]
        for t in range(2):
            polo[t, rows, :] = jnp.where(lane < LANES - ORIGIN, r[t], r[t + 1])

    def geometry(t, carry):
        for rt in range(2):
            base = 2 + 4 * rt
            here = [sgeo[HOME, t, k, pl.ds(base, 8), :] for k in range(4)]
            flags = [sword[HOME, t, k, pl.ds(base, 8), :] for k in range(3)]
            damped = here[3] * thole_damping
            for i, s in enumerate(SHIFTS):
                for j, dx in enumerate(SPAN[i]):
                    n = FIRST[i] + j
                    d = (dx, *s)
                    rows = pl.ds(base + dx, 8)
                    if d > (0, 0, 0):
                        c, m = FLAGS[d]
                        word = flags[c]
                    else:
                        c, m = FLAGS[tuple(-v for v in d)]
                        word = sword[i, t, c, rows, :]
                    present = (word & (1 << m)) != 0
                    sep = [
                        (sgeo[i, t, k, rows, :] - here[k]) + d[k] * site_spacing for k in range(3)
                    ]
                    sq = sep[0] * sep[0] + sep[1] * sep[1] + sep[2] * sep[2]
                    inv = lax.rsqrt(sq)
                    damp = (damped * sgeo[i, t, 3, rows, :]) * (sq * (sq * inv))
                    fall = jnp.exp(-damp)
                    inv2 = inv * inv
                    inv3 = inv2 * inv
                    iso = jnp.where(present, (1.0 - fall) * inv3, 0.0)
                    rad = jnp.where(present, (1.0 - (1.0 + damp) * fall) * (3.0 * inv3 * inv2), 0.0)
                    rs = [rad * v for v in sep]
                    coef[t, rt, n, 0] = rs[0] * sep[0] - iso
                    coef[t, rt, n, 1] = rs[0] * sep[1]
                    coef[t, rt, n, 2] = rs[0] * sep[2]
                    coef[t, rt, n, 3] = rs[1] * sep[1] - iso
                    coef[t, rt, n, 4] = rs[1] * sep[2]
                    coef[t, rt, n, 5] = rs[2] * sep[2] - iso
        return carry

    lax.fori_loop(0, 2, geometry, 0)

    def dots_start(index, vectors, number):
        line = jnp.zeros((1, LANES), f32)
        for m in range(number):
            value = weight * vectors[m // 2] * vectors[(m + 1) // 2]
            value = jnp.sum(jnp.sum(value, axis=0, keepdims=True), axis=1, keepdims=True)
            line = jnp.where(pick == m, value, line)
        dot_src[index] = line
        dot_dst[index, rank] = line
        for o in others:
            pltpu.make_async_remote_copy(
                src_ref=dot_src.at[index], dst_ref=dot_dst.at[index, rank],
                send_sem=dot_send.at[index], recv_sem=dot_recv.at[index],
                device_id=at(*o), device_id_type=MESH,
            ).start()

    def dots_all(index):
        some = dot_dst.at[index, pl.ds(0, count - 1)]
        return pltpu.make_async_remote_copy(
            src_ref=some, dst_ref=some, send_sem=dot_send.at[index], recv_sem=dot_recv.at[index],
            device_id=at(1, 0, 0), device_id_type=MESH,
        )

    def dots_finish(index, number):
        dots_all(index).wait_recv()
        line = jnp.sum(dot_dst[index, :, 0, :], axis=0, keepdims=True)
        return [
            jnp.broadcast_to(jnp.sum(jnp.where(pick == m, line, 0.0), axis=1, keepdims=True), (ROWS, LANES))
            for m in range(number)
        ]

    def scalars(moments, history, steps):
        number = 2 * steps
        before = [0.0] * number
        if history:
            _, _, mu1, eta1, inv1, _ = history[-1]
            _, _, mu2, eta2, inv2, _ = history[-2]
            before[1] = moments[0] * inv1
            before[2] = moments[1] * inv1 + mu1 * before[1]
            older2 = before[1] * inv2
            before[3] = moments[2] * inv1 + mu1 * before[2] + eta1 * older2
            older3 = before[2] * inv2 + mu2 * older2
            before[4] = moments[3] * inv1 + mu1 * before[3] + eta1 * older3
        now, lead, seen = list(moments), None, 0.0
        out = []
        known = list(history)
        for i in range(steps):
            gamma = now[i] if lead is None else lead * now[i]
            if known:
                eta = gamma * known[-1][4] / known[-1][5]
                beta = eta * known[-1][0]
            else:
                eta = beta = jnp.zeros((ROWS, LANES), f32)
            ratio = now[i + 1] / now[i]
            mu = ratio - seen
            seen = ratio
            inv = 1.0 - mu - eta
            alpha = 1.0 / inv
            later = [0.0] * number
            for m in range(i + 1, number - 1 - i):
                later[m] = alpha * (now[m + 1] - mu * now[m] - eta * before[m])
            before, now = now, later
            lead = alpha if lead is None else lead * alpha
            out.append((alpha, beta, mu, eta, inv, gamma))
            known.append(out[-1])
        return out

    def advance(values, old, cs, history):
        zm, cm, cmm = old
        (a0, _, m0, e0, _, _), (a1, _, m1, e1, _, _) = cs[:2]
        z0, v1, v2 = values[:3]
        if zm is None:
            z1 = a0 * (v1 - m0 * z0)
            c1 = a0 * (v2 - m0 * v1)
        else:
            z1 = a0 * (v1 - m0 * z0 - e0 * zm)
            c1 = a0 * (v2 - m0 * v1 - e0 * cm)
        z2 = a1 * (c1 - m1 * z1 - e1 * z0)
        if len(cs) == 2:
            return [z1, z2], (z1, c1, v1)
        v3 = values[3]
        a2, _, m2, e2, _, _ = cs[2]
        _, _, mu1, eta1, inv1, _ = history[-1]
        ccm = v1 * inv1 + mu1 * cm + eta1 * cmm
        cc1 = a0 * (v3 - m0 * v2 - e0 * ccm)
        c2 = a1 * (cc1 - m1 * c1 - e1 * v1)
        z3 = a2 * (c2 - m2 * z2 - e2 * z1)
        return [z1, z2, z3], (z2, c2, c1)

    line = jnp.zeros((1, LANES), f32)
    history = []
    pending = []
    p = None
    for index, steps in enumerate(BLOCKS):
        final = index == len(BLOCKS) - 1
        if index == 0:
            apply(None, 0, False)
            apply(0, 1, False)
            apply(1, 2, True)
            mine = [pack(0), pack(1), pack(2)]
            sent = mine
        else:
            apply(None, 1, False)
            apply(1, 2, False)
            apply(2, 3, True)
            mine = [z, pack(1), pack(2), pack(3)]
            sent = mine[1:]
        dots_start(index, mine, 2 * steps)
        if not final:
            for k in range(3):
                send1[index, k] = sent[k]
                recv1[index, own, k] = sent[k]
            copies = halo_start(1 + index, send1.at[index], recv1.at[index])
            pending.append(copies)
            for copy in copies:
                copy.wait_recv()
        moments = dots_finish(index, 2 * steps)
        cs = scalars(moments, history, steps)
        if not final:
            for b in range(18):
                got = [recv1[index, b, k] for k in range(3)]
                if index == 0:
                    values, old = got, (None, None, None)
                else:
                    values = [state[0, b], *got]
                    old = (state[1, b], state[2, b], state[3, b])
                zs, new = advance(values, old, cs, history)
                if b == own:
                    mine_z = zs
                    z_start = values[0]
                state[0, b] = zs[-1]
                for k in range(3):
                    state[1 + k, b] = new[k]
            for k in range(3):
                assemble(lambda b: state[0, b], k, ext.at[k])
            z = mine_z[-1]
        else:
            mine_z, _ = advance(mine, (state[1, own], state[2, own], state[3, own]), cs, history)
            z_start = mine[0]
        for i in range(steps):
            before = z_start if i == 0 else mine_z[i - 1]
            alpha, beta = cs[i][0], cs[i][1]
            p = before if p is None else before + beta * p
            x = x + alpha * p
            line = jnp.where(pick == len(history) + i, alpha[0:1], line)
        history = history + cs

    residual = mine_z[-1] * weight
    for y in range(EDGE):
        for c in range(3):
            shift = -(y * WIDE + c * EDGE)
            x_out[:, y, c, :] = roll(x, shift)[:EDGE, :EDGE]
            r_out[:, y, c, :] = roll(residual, shift)[:EDGE, :EDGE]
    len_out[...] = line

    for copy in copies0:
        copy.wait_send()
    for copies in pending:
        for copy in copies:
            copy.wait_send()
    for index in range(len(BLOCKS)):
        dots_all(index).wait_send()


def solution(mesh):
    sizes = tuple(mesh.shape[a] for a in ("gx", "gy", "gz"))
    assert sizes[0] == 2
    count = sizes[0] * sizes[1] * sizes[2]

    def local(permanent_field, polar, jitter, neighbors):
        assert polar.shape == (EDGE, EDGE, EDGE)
        vmem = pl.BlockSpec(memory_space=pltpu.VMEM)
        shape = jax.ShapeDtypeStruct((EDGE, EDGE, 3, EDGE), f32)
        wide, near = (3, 16, LANES), (2, 16, LANES)
        shifts = len(SHIFTS)
        x, r, steps = pl.pallas_call(
            functools.partial(kernel, sizes),
            out_shape=(shape, shape, jax.ShapeDtypeStruct((1, LANES), f32)),
            in_specs=[vmem] * 4,
            out_specs=(vmem, vmem, vmem),
            scratch_shapes=[
                pltpu.VMEM((3, *wide), f32),
                pltpu.VMEM((shifts, 2, 3, 16, LANES), f32),
                pltpu.VMEM((5, *wide), f32),
                pltpu.VMEM((3, *wide), f32),
                pltpu.VMEM((shifts, 2, 4, 16, LANES), f32),
                pltpu.VMEM((shifts, 2, 3, 16, LANES), jnp.int32),
                pltpu.VMEM(near, f32),
                pltpu.VMEM((2, 2, len(STENCIL), 6, ROWS, LANES), f32),
                pltpu.VMEM((4, 3, *near), f32),
                pltpu.VMEM((4, 18, ROWS, LANES), f32),
                pltpu.VMEM((TILES, ROWS, LANES), f32),
                pltpu.VMEM((18, TILES, ROWS, LANES), f32),
                pltpu.VMEM((2, 3, ROWS, LANES), f32),
                pltpu.VMEM((2, 18, 3, ROWS, LANES), f32),
                pltpu.VMEM((3, 1, LANES), f32),
                pltpu.VMEM((3, count, 1, LANES), f32),
                pltpu.SemaphoreType.DMA((3, 18)),
                pltpu.SemaphoreType.DMA((3, 18)),
                pltpu.SemaphoreType.DMA((3,)),
                pltpu.SemaphoreType.DMA((3,)),
            ],
            compiler_params=pltpu.CompilerParams(collective_id=0, has_side_effects=True),
        )(
            jnp.moveaxis(permanent_field, -1, 2),
            polar,
            jnp.moveaxis(jitter, -1, 2),
            neighbors,
        )
        return jnp.moveaxis(x, 2, -1), jnp.moveaxis(r, 2, -1), steps[0, :ITERS]

    return jax.shard_map(
        local,
        mesh=mesh,
        in_specs=(
            P("gx", "gy", "gz", None),
            P("gx", "gy", "gz"),
            P("gx", "gy", "gz", None),
            P("gx", "gy", "gz", None),
        ),
        out_specs=(P("gx", "gy", "gz", None), P("gx", "gy", "gz", None), P()),
        check_vma=False,
    )
```

time: 98.9 us -> 65.4 us (0.66)
  Pallas kernels: 90.2 us -> 61.3 us
  local copies, waits for them, and re-layouts: 6.6 us -> 3.32 us
  other arithmetic: 0.99 us -> 0 us
    pallas_call x1, Pallas kernels: 90.2 us -> 61.3 us  [local(): pl.pallas_call(functools.partial(kernel, sizes), out_shape=(shape, shape,...]
    pad x4 -> x0, local copies, waits for them, and re-layouts: 1.5 us -> none  [the longest x2 1.32 us: spread(): jnp.pad(array, ((0, 0), (0, 0), (0, LANES - wide * wide)), constant_value...]
    slice x1 -> x0, local copies, waits for them, and re-layouts: 1.31 us -> none  [local(): return (gather(x), gather(r), steps[:, 0])]
    unnamed x10 -> x6, local copies, waits for them, and re-layouts: 2.3 us -> 2.81 us
where the time goes in v1:
time: 65.4 us; the launch traced here: 65.3 us
  Pallas kernels  61.3 us (94%)
  local copies, waits for them, and re-layouts  3.32 us (5%)
    pallas_call x1, Pallas kernels, local(): pl.pallas_call(functools.partial(kernel, sizes), out_shape=(shape, shape,...  61.3 us
    unnamed x6, local copies, waits for them, and re-layouts  2.81 us

profile of v1, /device:TPU:1, one launch (start us, length us, event | category | flops | bytes accessed | tf_op | source)
XLA Modules:
  0.0 65.3 jit_solution(8592563039120432986)
XLA Ops:
  0.6 61.3 %shard_map.67 = (f32[6,6,3,6]{3,2,1,0:T(4,128)}, f32[6,6,3,6]{3,2,1,0:T(4,128)}, f32[1,128]{1,0:T(1,128)}) custom-call(f32[6,6,3,6]{3,2,1,0:T(4,128)} %bitcast.6, f32[6,6,6]{2,1,0:T(8,128)} %pol_ref.1, f32[6,6,3,6]{3,2,1,0:T(4,128)} %bitcast.7, s32[6,6,6,56]{3,2,1,0:T(8,128)} %nb_ref.1), custom_call_target="tpu_custom_call" | custom-call | tf_op jit(solution)/shard_map/pallas_call | solution.py:519
  61.9 0.0 copy-start.1
  61.9 0.6 copy-done.1
  62.5 0.5 slice_bitcast_fusion
  63.1 0.0 copy-start
  63.1 1.6 %copy.9 = f32[6,6,6,3]{2,3,1,0:T(4,128)} copy(f32[6,6,6,3]{2,3,1,0:T(4,128)} %bitcast.9) | data formatting | bytes 5184
  64.6 0.0 copy-done
  64.6 0.6 copy.10
Async XLA Ops:
  61.9 0.6 copy-start.1
  63.1 1.6 %copy-start = (f32[6,6,3,6]{3,2,1,0:T(4,128)S(1)}, f32[6,6,3,6]{3,2,1,0:T(4,128)}, u32[]{:S(2)}) copy-start(f32[6,6,3,6]{3,2,1,0:T(4,128)} %get-tuple-element.7) | copy-start | bytes 7780

commit v2 on v1

--- a/solution.py
+++ b/solution.py
@@ -59,10 +59,11 @@
 
 def kernel(
     sizes,
-    field_ref, pol_ref, jit_ref, nb_ref, x_out, r_out, len_out,
+    field_in, pol_in, jit_in, nb_in, out_ref,
+    field_ref, pol_ref, jit_ref, nb_ref,
     ext, sh, geo, words, sgeo, sword, polo, coef, chain, state,
     send0, recv0, send1, recv1, dot_src, dot_dst,
-    halo_send, halo_recv, dot_send, dot_recv,
+    halo_send, halo_recv, dot_send, dot_recv, in_sems,
 ):
     nx, ny, nz = sizes
     count = nx * ny * nz
@@ -80,6 +81,14 @@
     barrier = pltpu.get_barrier_semaphore()
     for o in others:
         pl.semaphore_signal(barrier, inc=1, device_id=at(*o), device_id_type=MESH)
+    loads = [
+        pltpu.make_async_copy(source, target, in_sems.at[k])
+        for k, (source, target) in enumerate((
+            (nb_in, nb_ref), (field_in, field_ref), (pol_in, pol_ref), (jit_in, jit_ref),
+        ))
+    ]
+    for load in loads:
+        load.start()
 
     lane = lax.broadcasted_iota(jnp.int32, (ROWS, LANES), 1)
     row = lax.broadcasted_iota(jnp.int32, (ROWS, LANES), 0)
@@ -103,6 +112,8 @@
                 out = out + roll(part, y * WIDE + c * EDGE)
         return out
 
+    for load in loads:
+        load.wait()
     field, jit = gather3(field_ref, 3), gather3(jit_ref, 3) * site_spacing
     pol0 = gather3(pol_ref, 1)
     polp = pol0 + roll(pol0, EDGE) + roll(pol0, 2 * EDGE)
@@ -147,7 +158,7 @@
     own = 4
     recv0[own] = send0[...]
 
-    def halo_start(index, src, dst):
+    def halo_start(index, src, get_dst):
         copies = []
         for oy in (-1, 1, 0):
             for oz in (-1, 1, 0):
@@ -158,7 +169,7 @@
                     here = ox * 9 + (1 + oy) * 3 + 1 + oz
                     copies.append(
                         pltpu.make_async_remote_copy(
-                            src_ref=src, dst_ref=dst.at[back],
+                            src_ref=src, dst_ref=get_dst(back),
                             send_sem=halo_send.at[index, here], recv_sem=halo_recv.at[index, back],
                             device_id=at(ox, oy, oz), device_id_type=MESH,
                         )
@@ -185,68 +196,62 @@
             target[t, 0:2, :] = full[1][t][4:6]
             target[t, 14:16, :] = full[0][t][:2]
 
-    def wide_shift(get, put):
-        for half in range(2):
-            rows = pl.ds(8 * half, 8)
-            v = [get(t, rows) for t in range(3)]
-            for i, (dy, dz) in enumerate(SHIFTS):
-                a = ORIGIN + dy * WIDE + dz
-                r = [roll(u, -a) for u in v]
-                for t in range(2):
-                    put(i, t, rows, jnp.where(lane < LANES - a, r[t], r[t + 1]))
-
-    def near_shift(get, put):
-        for half in range(2):
-            rows = pl.ds(8 * half, 8)
-            v = [get(t, rows) for t in range(2)]
-            for i, (dy, dz) in enumerate(SHIFTS):
-                s = dy * WIDE + dz
-                r = [roll(u, -s) for u in v]
-                if s > 0:
-                    r[0] = jnp.where(lane < LANES - s, r[0], r[1])
-                elif s < 0:
-                    r[1] = jnp.where(lane >= -s, r[1], r[0])
-                for t in range(2):
-                    put(i, t, rows, r[t])
+    def shifted(v, i):
+        dy, dz = SHIFTS[i]
+        s = dy * WIDE + dz + (ORIGIN if len(v) == 3 else 0)
+        if s == 0:
+            return v
+        r = [roll(u, -s) for u in v]
+        if len(v) == 3:
+            return [jnp.where(lane < LANES - s, r[t], r[t + 1]) for t in range(2)]
+        if s > 0:
+            return [jnp.where(lane < LANES - s, r[0], r[1]), r[1]]
+        return [r[0], jnp.where(lane >= -s, r[1], r[0])]
+
+    halves = (pl.ds(0, 8), pl.ds(8, 8))
 
     def apply(source, target, last):
-        def shift(k, carry):
-            def put(i, t, rows, value):
-                sh[i, t, k, rows, :] = value
-
-            if source is None:
-                wide_shift(lambda t, rows: ext[k, t, rows, :], put)
-            else:
-                near_shift(lambda t, rows: chain[source, k, t, rows, :], put)
-            return carry
-
-        lax.fori_loop(0, 3, shift, 0)
-
-        def tile(t, carry):
-            for rt in range(1 if last else 2):
-                acc = [[None, None] for _ in range(3)]
-                for i in range(len(SHIFTS)):
-                    for j, dx in enumerate(SPAN[i]):
-                        n = FIRST[i] + j
-                        a, b, c = [sh[i, t, k, pl.ds(dx + 2 + 4 * rt, 8), :] for k in range(3)]
-                        xx, xy, xz, yy, yz, zz = [coef[t, rt, n, k] for k in range(6)]
-                        for k, term in enumerate((
-                            xx * a + xy * b + xz * c, xy * a + yy * b + yz * c, xz * a + yz * b + zz * c,
-                        )):
-                            old = acc[k][n % 2]
-                            acc[k][n % 2] = term if old is None else old + term
-                scale = polo[t, pl.ds(2 + 4 * rt, 8), :]
-                for k in range(3):
-                    out = (acc[k][0] + acc[k][1]) * scale
-                    chain[target, k, t, pl.ds(2 + 4 * rt, 8), :] = out
-                    if not last:
-                        if rt == 0:
-                            chain[target, k, t, 14:16, :] = out[0:2]
-                        else:
-                            chain[target, k, t, 0:2, :] = out[6:8]
-            return carry
-
-        lax.fori_loop(0, 2, tile, 0)
+        tiles = range(3) if source is None else range(2)
+
+        def shift(i):
+            for k in range(3):
+                for rows in halves:
+                    ref = ext.at[k] if source is None else chain.at[source, k]
+                    for t, value in enumerate(shifted([ref[t, rows, :] for t in tiles], i)):
+                        sh[i, t, k, rows, :] = value
+
+        sides = [(t, rt) for t in range(2) for rt in range(1 if last else 2)]
+        acc = {side: [None] * 3 for side in sides}
+
+        def compute(i):
+            for j, dx in enumerate(SPAN[i]):
+                n = FIRST[i] + j
+                for t, rt in sides:
+                    v = [sh[i, t, k, pl.ds(dx + 2 + 4 * rt, 8), :] for k in range(3)]
+                    u = [coef[t, rt, n, k] for k in range(3)]
+                    iso = coef[t, rt, n, 3]
+                    dot = u[0] * v[0] + u[1] * v[1] + u[2] * v[2]
+                    for k in range(3):
+                        term = u[k] * dot - iso * v[k]
+                        old = acc[t, rt][k]
+                        acc[t, rt][k] = term if old is None else old + term
+
+        ahead = 4
+        for i in range(len(SHIFTS) + ahead):
+            if i < len(SHIFTS):
+                shift(i)
+            if i >= ahead:
+                compute(i - ahead)
+        for t, rt in sides:
+            scale = polo[t, pl.ds(2 + 4 * rt, 8), :]
+            for k in range(3):
+                out = acc[t, rt][k] * scale
+                chain[target, k, t, pl.ds(2 + 4 * rt, 8), :] = out
+                if not last:
+                    if rt == 0:
+                        chain[target, k, t, 14:16, :] = out[0:2]
+                    else:
+                        chain[target, k, t, 0:2, :] = out[6:8]
 
     def pack(index):
         parts = []
@@ -258,7 +263,7 @@
         return jnp.where(packed, out, 0.0)
 
     pl.semaphore_wait(barrier, len(others))
-    copies0 = halo_start(0, send0, recv0)
+    copies0 = halo_start(0, send0, lambda b: recv0.at[b])
     chain[...] = jnp.zeros_like(chain)
     for copy in copies0:
         copy.wait_recv()
@@ -279,23 +284,14 @@
     for k in range(3):
         assemble(lambda b: state[0, b], k, words.at[k])
 
-    def shift_geo(k, carry):
-        def put(i, t, rows, value):
-            sgeo[i, t, k, rows, :] = value
-
-        wide_shift(lambda t, rows: geo[k, t, rows, :], put)
-        return carry
-
-    lax.fori_loop(0, 4, shift_geo, 0)
-
-    def shift_words(k, carry):
-        def put(i, t, rows, value):
-            sword[i, t, k, rows, :] = value.astype(jnp.int32)
-
-        wide_shift(lambda t, rows: words[k, t, rows, :], put)
-        return carry
-
-    lax.fori_loop(0, 3, shift_words, 0)
+    for i in range(len(SHIFTS)):
+        for rows in halves:
+            for k in range(4):
+                for t, value in enumerate(shifted([geo[k, t, rows, :] for t in range(3)], i)):
+                    sgeo[i, t, k, rows, :] = value
+            for k in range(3):
+                for t, value in enumerate(shifted([words[k, t, rows, :] for t in range(3)], i)):
+                    sword[i, t, k, rows, :] = value.astype(jnp.int32)
     for half in range(2):
         rows = pl.ds(8 * half, 8)
         r = [roll(geo[4, t, rows, :], -ORIGIN) for t in range(3)]
@@ -320,9 +316,8 @@
                         c, m = FLAGS[tuple(-v for v in d)]
                         word = sword[i, t, c, rows, :]
                     present = (word & (1 << m)) != 0
-                    sep = [
-                        (sgeo[i, t, k, rows, :] - here[k]) + d[k] * site_spacing for k in range(3)
-                    ]
+                    sep = [sgeo[i, t, k, rows, :] - here[k] for k in range(3)]
+                    sep = [v + e * site_spacing if e else v for v, e in zip(sep, d)]
                     sq = sep[0] * sep[0] + sep[1] * sep[1] + sep[2] * sep[2]
                     inv = lax.rsqrt(sq)
                     damp = (damped * sgeo[i, t, 3, rows, :]) * (sq * (sq * inv))
@@ -330,14 +325,11 @@
                     inv2 = inv * inv
                     inv3 = inv2 * inv
                     iso = jnp.where(present, (1.0 - fall) * inv3, 0.0)
-                    rad = jnp.where(present, (1.0 - (1.0 + damp) * fall) * (3.0 * inv3 * inv2), 0.0)
-                    rs = [rad * v for v in sep]
-                    coef[t, rt, n, 0] = rs[0] * sep[0] - iso
-                    coef[t, rt, n, 1] = rs[0] * sep[1]
-                    coef[t, rt, n, 2] = rs[0] * sep[2]
-                    coef[t, rt, n, 3] = rs[1] * sep[1] - iso
-                    coef[t, rt, n, 4] = rs[1] * sep[2]
-                    coef[t, rt, n, 5] = rs[2] * sep[2] - iso
+                    rad = (1.0 - (1.0 + damp) * fall) * (3.0 * inv3 * inv2)
+                    root = jnp.where(present, rad * lax.rsqrt(rad), 0.0)
+                    for k in range(3):
+                        coef[t, rt, n, k] = root * sep[k]
+                    coef[t, rt, n, 3] = iso
         return carry
 
     lax.fori_loop(0, 2, geometry, 0)
@@ -436,27 +428,26 @@
     p = None
     for index, steps in enumerate(BLOCKS):
         final = index == len(BLOCKS) - 1
-        if index == 0:
-            apply(None, 0, False)
-            apply(0, 1, False)
-            apply(1, 2, True)
-            mine = [pack(0), pack(1), pack(2)]
-            sent = mine
-        else:
-            apply(None, 1, False)
-            apply(1, 2, False)
-            apply(2, 3, True)
-            mine = [z, pack(1), pack(2), pack(3)]
-            sent = mine[1:]
+        copies = []
+
+        def share(k, value):
+            if not final:
+                send1[index, k] = value
+                recv1[index, own, k] = value
+                copies.extend(halo_start(
+                    1 + 3 * index + k, send1.at[index, k], lambda b: recv1.at[index, b, k]
+                ))
+            return value
+
+        start = 0 if index == 0 else 1
+        mine = [] if index == 0 else [z]
+        for k in range(3):
+            apply(None if k == 0 else start + k - 1, start + k, k == 2)
+            mine.append(share(k, pack(start + k)))
         dots_start(index, mine, 2 * steps)
-        if not final:
-            for k in range(3):
-                send1[index, k] = sent[k]
-                recv1[index, own, k] = sent[k]
-            copies = halo_start(1 + index, send1.at[index], recv1.at[index])
-            pending.append(copies)
-            for copy in copies:
-                copy.wait_recv()
+        pending.append(copies)
+        for copy in copies:
+            copy.wait_recv()
         moments = dots_finish(index, 2 * steps)
         cs = scalars(moments, history, steps)
         if not final:
@@ -489,12 +480,9 @@
         history = history + cs
 
     residual = mine_z[-1] * weight
-    for y in range(EDGE):
-        for c in range(3):
-            shift = -(y * WIDE + c * EDGE)
-            x_out[:, y, c, :] = roll(x, shift)[:EDGE, :EDGE]
-            r_out[:, y, c, :] = roll(residual, shift)[:EDGE, :EDGE]
-    len_out[...] = line
+    out_ref[0] = x
+    out_ref[1] = residual
+    out_ref[2, 0:1, :] = line
 
     for copy in copies0:
         copy.wait_send()
@@ -505,6 +493,15 @@
         dots_all(index).wait_send()
 
 
+def unpack(in_ref, x_out, r_out, len_out):
+    for k, ref in enumerate((x_out, r_out)):
+        value = in_ref[k]
+        for y in range(EDGE):
+            for c in range(3):
+                ref[:, y, c, :] = roll(value, -(y * WIDE + c * EDGE))[:EDGE, :EDGE]
+    len_out[...] = in_ref[2, 0:1, :ITERS]
+
+
 def solution(mesh):
     sizes = tuple(mesh.shape[a] for a in ("gx", "gy", "gz"))
     assert sizes[0] == 2
@@ -516,12 +513,17 @@
         shape = jax.ShapeDtypeStruct((EDGE, EDGE, 3, EDGE), f32)
         wide, near = (3, 16, LANES), (2, 16, LANES)
         shifts = len(SHIFTS)
-        x, r, steps = pl.pallas_call(
+        anywhere = pl.BlockSpec(memory_space=pl.ANY)
+        packed = pl.pallas_call(
             functools.partial(kernel, sizes),
-            out_shape=(shape, shape, jax.ShapeDtypeStruct((1, LANES), f32)),
-            in_specs=[vmem] * 4,
-            out_specs=(vmem, vmem, vmem),
+            out_shape=jax.ShapeDtypeStruct((3, ROWS, LANES), f32),
+            in_specs=[anywhere] * 4,
+            out_specs=vmem,
             scratch_shapes=[
+                pltpu.VMEM((EDGE, EDGE, 3, EDGE), f32),
+                pltpu.VMEM((EDGE, EDGE, EDGE), f32),
+                pltpu.VMEM((EDGE, EDGE, 3, EDGE), f32),
+                pltpu.VMEM(neighbors.shape, jnp.int32),
                 pltpu.VMEM((3, *wide), f32),
                 pltpu.VMEM((shifts, 2, 3, 16, LANES), f32),
                 pltpu.VMEM((5, *wide), f32),
@@ -529,7 +531,7 @@
                 pltpu.VMEM((shifts, 2, 4, 16, LANES), f32),
                 pltpu.VMEM((shifts, 2, 3, 16, LANES), jnp.int32),
                 pltpu.VMEM(near, f32),
-                pltpu.VMEM((2, 2, len(STENCIL), 6, ROWS, LANES), f32),
+                pltpu.VMEM((2, 2, len(STENCIL), 4, ROWS, LANES), f32),
                 pltpu.VMEM((4, 3, *near), f32),
                 pltpu.VMEM((4, 18, ROWS, LANES), f32),
                 pltpu.VMEM((TILES, ROWS, LANES), f32),
@@ -538,10 +540,11 @@
                 pltpu.VMEM((2, 18, 3, ROWS, LANES), f32),
                 pltpu.VMEM((3, 1, LANES), f32),
                 pltpu.VMEM((3, count, 1, LANES), f32),
-                pltpu.SemaphoreType.DMA((3, 18)),
-                pltpu.SemaphoreType.DMA((3, 18)),
+                pltpu.SemaphoreType.DMA((7, 18)),
+                pltpu.SemaphoreType.DMA((7, 18)),
                 pltpu.SemaphoreType.DMA((3,)),
                 pltpu.SemaphoreType.DMA((3,)),
+                pltpu.SemaphoreType.DMA((4,)),
             ],
             compiler_params=pltpu.CompilerParams(collective_id=0, has_side_effects=True),
         )(
@@ -550,7 +553,13 @@
             jnp.moveaxis(jitter, -1, 2),
             neighbors,
         )
-        return jnp.moveaxis(x, 2, -1), jnp.moveaxis(r, 2, -1), steps[0, :ITERS]
+        x, r, steps = pl.pallas_call(
+            unpack,
+            out_shape=(shape, shape, jax.ShapeDtypeStruct((1, ITERS), f32)),
+            in_specs=[vmem],
+            out_specs=(vmem, vmem, vmem),
+        )(packed)
+        return jnp.moveaxis(x, 2, -1), jnp.moveaxis(r, 2, -1), steps.reshape(ITERS)
 
     return jax.shard_map(
         local,

time: 65.4 us -> 56.4 us (0.86)
  Pallas kernels: 61.3 us -> 55.6 us
  local copies, waits for them, and re-layouts: 3.32 us -> 0 us
    pallas_call x1 -> x2, Pallas kernels: 61.3 us -> 55.6 us  [the longest x1 54.2 us: local(): pl.pallas_call(functools.partial(kernel, sizes), out_shape=jax.ShapeDtype...]
    unnamed x6 -> x0, local copies, waits for them, and re-layouts: 2.81 us -> none
where the time goes in v2:
time: 56.4 us; the launch traced here: 56.3 us
  Pallas kernels  55.6 us (99%)
  between operations  0.64 us (1%)
    pallas_call x1, Pallas kernels, local(): pl.pallas_call(functools.partial(kernel, sizes), out_shape=jax.ShapeDtype...  54.2 us
    pallas_call x1, Pallas kernels, local(): pl.pallas_call(unpack, out_shape=(shape, shape, jax.ShapeDtypeStruct((1,...  1.47 us

profile of v2, /device:TPU:1, one launch (start us, length us, event | category | flops | bytes accessed | tf_op | source)
XLA Modules:
  0.0 56.3 jit_solution(10058726874766739091)
XLA Ops:
  0.6 54.2 %shard_map.67.in_ref = f32[3,8,128]{2,1,0:T(8,128)} custom-call(f32[6,6,3,6]{3,2,1,0:T(4,128)} %bitcast.5, f32[6,6,6]{2,1,0:T(8,128)} %pol_in.1, f32[6,6,3,6]{3,2,1,0:T(4,128)} %bitcast.6, s32[6,6,6,56]{3,2,1,0:T(8,128)} %nb_in.1), custom_call_target="tpu_custom_call" | custom-call | tf_op jit(solution)/shard_map/pallas_call | solution.py:517
  54.8 1.5 %shard_map.68 = (f32[6,6,3,6]{3,2,1,0:T(4,128)}, f32[6,6,3,6]{3,2,1,0:T(4,128)}, f32[1,8]{1,0:T(1,128)}) custom-call(f32[3,8,128]{2,1,0:T(8,128)} %shard_map.67.in_ref), custom_call_target="tpu_custom_call" | custom-call | tf_op jit(solution)/shard_map/pallas_call | solution.py:556

commit v3 on v2

--- a/solution.py
+++ b/solution.py
@@ -8,7 +8,6 @@
 from jax.sharding import PartitionSpec as P
 
 ITERS = 8
-BLOCKS = (2, 3, 3)
 MESH = pl.DeviceIdType.MESH
 thole_damping = 0.39
 site_spacing = 3.5
@@ -61,7 +60,7 @@
     sizes,
     field_in, pol_in, jit_in, nb_in, out_ref,
     field_ref, pol_ref, jit_ref, nb_ref,
-    ext, sh, geo, words, sgeo, sword, polo, coef, chain, state,
+    ext, sh, geo, words, sgeo, sword, polo, coef, chain,
     send0, recv0, send1, recv1, dot_src, dot_dst,
     halo_send, halo_recv, dot_send, dot_recv, in_sems,
 ):
@@ -158,25 +157,28 @@
     own = 4
     recv0[own] = send0[...]
 
+    real = pl.ds(0, EDGE)
+
     def halo_start(index, src, get_dst):
-        copies = []
         for oy in (-1, 1, 0):
             for oz in (-1, 1, 0):
                 for ox in (1, 0):
                     if (ox, oy, oz) == (0, 0, 0):
                         continue
                     back = ox * 9 + (1 - oy) * 3 + 1 - oz
-                    here = ox * 9 + (1 + oy) * 3 + 1 + oz
-                    copies.append(
-                        pltpu.make_async_remote_copy(
-                            src_ref=src, dst_ref=get_dst(back),
-                            send_sem=halo_send.at[index, here], recv_sem=halo_recv.at[index, back],
-                            device_id=at(ox, oy, oz), device_id_type=MESH,
-                        )
-                    )
-        for copy in copies:
-            copy.start()
-        return copies
+                    pltpu.make_async_remote_copy(
+                        src_ref=src, dst_ref=get_dst(back),
+                        send_sem=halo_send.at[index], recv_sem=halo_recv.at[index],
+                        device_id=at(ox, oy, oz), device_id_type=MESH,
+                    ).start()
+
+    def halo_all(index):
+        some = pl.ds(0, 17)
+        ref = recv0.at[some, :, real] if index == 0 else recv1.at[index - 1, some, real]
+        return pltpu.make_async_remote_copy(
+            src_ref=ref, dst_ref=ref, send_sem=halo_send.at[index], recv_sem=halo_recv.at[index],
+            device_id=at(1, 0, 0), device_id_type=MESH,
+        )
 
     def assemble(get, c, target, fill=0.0):
         full = []
@@ -263,10 +265,9 @@
         return jnp.where(packed, out, 0.0)
 
     pl.semaphore_wait(barrier, len(others))
-    copies0 = halo_start(0, send0, lambda b: recv0.at[b])
+    halo_start(0, send0.at[:, real], lambda b: recv0.at[b, :, real])
     chain[...] = jnp.zeros_like(chain)
-    for copy in copies0:
-        copy.wait_recv()
+    halo_all(0).wait_recv()
 
     for k in range(3):
         assemble(lambda b: recv0[b, 0], k, geo.at[k])
@@ -279,10 +280,8 @@
     for n in range(FLAG_TILES):
         for b in range(18):
             flagged[b] = flagged[b] + recv0[b, 3 + n] * float(2 ** n)
-    for b in range(18):
-        state[0, b] = flagged[b]
     for k in range(3):
-        assemble(lambda b: state[0, b], k, words.at[k])
+        assemble(lambda b: flagged[b], k, words.at[k])
 
     for i in range(len(SHIFTS)):
         for rows in halves:
@@ -400,96 +399,69 @@
             known.append(out[-1])
         return out
 
-    def advance(values, old, cs, history):
-        zm, cm, cmm = old
-        (a0, _, m0, e0, _, _), (a1, _, m1, e1, _, _) = cs[:2]
-        z0, v1, v2 = values[:3]
-        if zm is None:
-            z1 = a0 * (v1 - m0 * z0)
-            c1 = a0 * (v2 - m0 * v1)
-        else:
-            z1 = a0 * (v1 - m0 * z0 - e0 * zm)
-            c1 = a0 * (v2 - m0 * v1 - e0 * cm)
-        z2 = a1 * (c1 - m1 * z1 - e1 * z0)
-        if len(cs) == 2:
-            return [z1, z2], (z1, c1, v1)
-        v3 = values[3]
-        a2, _, m2, e2, _, _ = cs[2]
-        _, _, mu1, eta1, inv1, _ = history[-1]
-        ccm = v1 * inv1 + mu1 * cm + eta1 * cmm
-        cc1 = a0 * (v3 - m0 * v2 - e0 * ccm)
-        c2 = a1 * (cc1 - m1 * c1 - e1 * v1)
-        z3 = a2 * (c2 - m2 * z2 - e2 * z1)
-        return [z1, z2, z3], (z2, c2, c1)
+    known = []
+    table = [[]]
+
+    def lanczos(vectors):
+        i = len(table) - 1
+        alpha, _, mu, eta, _, _ = known[i]
+        now = table[i]
+        table.append([
+            alpha * (now[m + 1] - mu * now[m] - (eta * table[i - 1][m] if i else 0.0))
+            for m in range(vectors)
+        ])
+
+    def chain_of_three():
+        out = []
+        for k in range(3):
+            apply(None if k == 0 else k - 1, k, k == 2)
+            out.append(pack(k))
+        return out
+
+    def share(index, value):
+        send1[index] = value
+        recv1[index, own] = value
+        halo_start(1 + index, send1.at[index, real], lambda b: recv1.at[index, b, real])
+
+    def receive(index):
+        halo_all(1 + index).wait_recv()
+        for k in range(3):
+            assemble(lambda b: recv1[index, b], k, ext.at[k])
+
+    table[0] += chain_of_three()
+    share(0, table[0][2])
+    dots_start(0, table[0], 4)
+    receive(0)
+    table[0] += chain_of_three()
+    known += scalars(dots_finish(0, 4), known, 2)
+    lanczos(5)
+    lanczos(4)
+    share(1, table[2][3])
+    dots_start(1, table[2], 6)
+    receive(1)
+    table[2] += chain_of_three()
+    known += scalars(dots_finish(1, 6), known, 3)
+    table[1].append(table[2][4] * known[1][4] + known[1][2] * table[1][4] + known[1][3] * table[0][4])
+    for vectors in (6, 5, 4):
+        lanczos(vectors)
+    dots_start(2, table[5], 6)
+    known += scalars(dots_finish(2, 6), known, 3)
+    for vectors in (3, 2, 1):
+        lanczos(vectors)
 
     line = jnp.zeros((1, LANES), f32)
-    history = []
-    pending = []
     p = None
-    for index, steps in enumerate(BLOCKS):
-        final = index == len(BLOCKS) - 1
-        copies = []
-
-        def share(k, value):
-            if not final:
-                send1[index, k] = value
-                recv1[index, own, k] = value
-                copies.extend(halo_start(
-                    1 + 3 * index + k, send1.at[index, k], lambda b: recv1.at[index, b, k]
-                ))
-            return value
-
-        start = 0 if index == 0 else 1
-        mine = [] if index == 0 else [z]
-        for k in range(3):
-            apply(None if k == 0 else start + k - 1, start + k, k == 2)
-            mine.append(share(k, pack(start + k)))
-        dots_start(index, mine, 2 * steps)
-        pending.append(copies)
-        for copy in copies:
-            copy.wait_recv()
-        moments = dots_finish(index, 2 * steps)
-        cs = scalars(moments, history, steps)
-        if not final:
-            for b in range(18):
-                got = [recv1[index, b, k] for k in range(3)]
-                if index == 0:
-                    values, old = got, (None, None, None)
-                else:
-                    values = [state[0, b], *got]
-                    old = (state[1, b], state[2, b], state[3, b])
-                zs, new = advance(values, old, cs, history)
-                if b == own:
-                    mine_z = zs
-                    z_start = values[0]
-                state[0, b] = zs[-1]
-                for k in range(3):
-                    state[1 + k, b] = new[k]
-            for k in range(3):
-                assemble(lambda b: state[0, b], k, ext.at[k])
-            z = mine_z[-1]
-        else:
-            mine_z, _ = advance(mine, (state[1, own], state[2, own], state[3, own]), cs, history)
-            z_start = mine[0]
-        for i in range(steps):
-            before = z_start if i == 0 else mine_z[i - 1]
-            alpha, beta = cs[i][0], cs[i][1]
-            p = before if p is None else before + beta * p
-            x = x + alpha * p
-            line = jnp.where(pick == len(history) + i, alpha[0:1], line)
-        history = history + cs
-
-    residual = mine_z[-1] * weight
+    for i, (alpha, beta, *_) in enumerate(known):
+        p = table[i][0] if p is None else table[i][0] + beta * p
+        x = x + alpha * p
+        line = jnp.where(pick == i, alpha[0:1], line)
+    residual = table[ITERS][0] * weight
     out_ref[0] = x
     out_ref[1] = residual
     out_ref[2, 0:1, :] = line
 
-    for copy in copies0:
-        copy.wait_send()
-    for copies in pending:
-        for copy in copies:
-            copy.wait_send()
-    for index in range(len(BLOCKS)):
+    for index in range(3):
+        halo_all(index).wait_send()
         dots_all(index).wait_send()
 
 
@@ -516,7 +488,7 @@
         anywhere = pl.BlockSpec(memory_space=pl.ANY)
         packed = pl.pallas_call(
             functools.partial(kernel, sizes),
-            out_shape=jax.ShapeDtypeStruct((3, ROWS, LANES), f32),
+            out_shape=pltpu.VMEM((3, ROWS, LANES), f32),
             in_specs=[anywhere] * 4,
             out_specs=vmem,
             scratch_shapes=[
@@ -532,16 +504,15 @@
                 pltpu.VMEM((shifts, 2, 3, 16, LANES), jnp.int32),
                 pltpu.VMEM(near, f32),
                 pltpu.VMEM((2, 2, len(STENCIL), 4, ROWS, LANES), f32),
-                pltpu.VMEM((4, 3, *near), f32),
-                pltpu.VMEM((4, 18, ROWS, LANES), f32),
+                pltpu.VMEM((3, 3, *near), f32),
                 pltpu.VMEM((TILES, ROWS, LANES), f32),
                 pltpu.VMEM((18, TILES, ROWS, LANES), f32),
-                pltpu.VMEM((2, 3, ROWS, LANES), f32),
-                pltpu.VMEM((2, 18, 3, ROWS, LANES), f32),
+                pltpu.VMEM((2, ROWS, LANES), f32),
+                pltpu.VMEM((2, 18, ROWS, LANES), f32),
                 pltpu.VMEM((3, 1, LANES), f32),
                 pltpu.VMEM((3, count, 1, LANES), f32),
-                pltpu.SemaphoreType.DMA((7, 18)),
-                pltpu.SemaphoreType.DMA((7, 18)),
+                pltpu.SemaphoreType.DMA((3,)),
+                pltpu.SemaphoreType.DMA((3,)),
                 pltpu.SemaphoreType.DMA((3,)),
                 pltpu.SemaphoreType.DMA((3,)),
                 pltpu.SemaphoreType.DMA((4,)),
@@ -558,7 +529,7 @@
             out_shape=(shape, shape, jax.ShapeDtypeStruct((1, ITERS), f32)),
             in_specs=[vmem],
             out_specs=(vmem, vmem, vmem),
-        )(packed)
+        )(pltpu.with_memory_space_constraint(packed, pltpu.VMEM))
         return jnp.moveaxis(x, 2, -1), jnp.moveaxis(r, 2, -1), steps.reshape(ITERS)
 
     return jax.shard_map(

time: 56.4 us -> 48.5 us (0.86)
  Pallas kernels: 55.6 us -> 47.7 us
    pallas_call x1, Pallas kernels: 54.2 us -> 47 us  [local(): pl.pallas_call(functools.partial(kernel, sizes), out_shape=pltpu.VMEM((3,...]
    pallas_call x1, Pallas kernels: 1.47 us -> 0.77 us  [local(): pl.pallas_call(unpack, out_shape=(shape, shape, jax.ShapeDtypeStruct((1,...]
where the time goes in v3:
time: 48.5 us; the launch traced here: 48.4 us
  Pallas kernels  47.7 us (98%)
  between operations  0.64 us (1%)
    pallas_call x1, Pallas kernels, local(): pl.pallas_call(functools.partial(kernel, sizes), out_shape=pltpu.VMEM((3,...  47 us

profile of v3, /device:TPU:1, one launch (start us, length us, event | category | flops | bytes accessed | tf_op | source)
XLA Modules:
  0.0 48.4 jit_solution(13483236807321637954)
XLA Ops:
  0.6 47.0 %shard_map.67.in_ref = f32[3,8,128]{2,1,0:T(8,128)S(1)} custom-call(f32[6,6,3,6]{3,2,1,0:T(4,128)} %bitcast.5, f32[6,6,6]{2,1,0:T(8,128)} %pol_in.1, f32[6,6,3,6]{3,2,1,0:T(4,128)} %bitcast.6, s32[6,6,6,56]{3,2,1,0:T(8,128)} %nb_in.1), custom_call_target="tpu_custom_call" | custom-call | tf_op jit(solution)/shard_map/pallas_call | solution.py:489
  47.6 0.8 %shard_map.68 = (f32[6,6,3,6]{3,2,1,0:T(4,128)}, f32[6,6,3,6]{3,2,1,0:T(4,128)}, f32[1,8]{1,0:T(1,128)}) custom-call(f32[3,8,128]{2,1,0:T(8,128)S(1)} %shard_map.67.in_ref), custom_call_target="tpu_custom_call" | custom-call | tf_op jit(solution)/shard_map/pallas_call | solution.py:527

commit v4 on v3

--- a/solution.py
+++ b/solution.py
@@ -48,7 +48,9 @@
 
 FLAGS = flag_places()
 FLAG_TILES = 9
-TILES = 3 + FLAG_TILES
+TILES = 3
+GREET_Y = (0, 1, 3)
+GREET_Z = (0, 1, 4, 7, 9, 12, 15)
 
 
 def roll(value, shift):
@@ -61,7 +63,7 @@
     field_in, pol_in, jit_in, nb_in, out_ref,
     field_ref, pol_ref, jit_ref, nb_ref,
     ext, sh, geo, words, sgeo, sword, polo, coef, chain,
-    send0, recv0, send1, recv1, dot_src, dot_dst,
+    send0, recv0, sendf, recvf, send1, recv1, dot_src, dot_dst,
     halo_send, halo_recv, dot_send, dot_recv, in_sems,
 ):
     nx, ny, nz = sizes
@@ -78,8 +80,6 @@
     others.sort(key=lambda o: -(min(o[0], nx - o[0]) + 2 * min(o[1], ny - o[1]) + 2 * min(o[2], nz - o[2])))
 
     barrier = pltpu.get_barrier_semaphore()
-    for o in others:
-        pl.semaphore_signal(barrier, inc=1, device_id=at(*o), device_id_type=MESH)
     loads = [
         pltpu.make_async_copy(source, target, in_sems.at[k])
         for k, (source, target) in enumerate((
@@ -88,7 +88,9 @@
     ]
     for load in loads:
         load.start()
-
+    greeted = [o for o in others if o[1] in GREET_Y and o[2] in GREET_Z]
+    for o in greeted:
+        pl.semaphore_signal(barrier, inc=1, device_id=at(*o), device_id_type=MESH)
     lane = lax.broadcasted_iota(jnp.int32, (ROWS, LANES), 1)
     row = lax.broadcasted_iota(jnp.int32, (ROWS, LANES), 0)
     pick = lax.broadcasted_iota(jnp.int32, (1, LANES), 1)
@@ -153,9 +155,10 @@
     send0[1] = x
     send0[2] = pol0 + flag_tile(FLAG_TILES)
     for n in range(FLAG_TILES):
-        send0[3 + n] = flag_tile(n)
+        sendf[n] = flag_tile(n)
     own = 4
     recv0[own] = send0[...]
+    recvf[own] = sendf[...]
 
     real = pl.ds(0, EDGE)
 
@@ -174,7 +177,10 @@
 
     def halo_all(index):
         some = pl.ds(0, 17)
-        ref = recv0.at[some, :, real] if index == 0 else recv1.at[index - 1, some, real]
+        ref = {
+            0: recv0.at[some, :, real], 3: recvf.at[some, :, real],
+            1: recv1.at[0, some, real], 2: recv1.at[1, some, real],
+        }[index]
         return pltpu.make_async_remote_copy(
             src_ref=ref, dst_ref=ref, send_sem=halo_send.at[index], recv_sem=halo_recv.at[index],
             device_id=at(1, 0, 0), device_id_type=MESH,
@@ -212,7 +218,15 @@
 
     halves = (pl.ds(0, 8), pl.ds(8, 8))
 
-    def apply(source, target, last):
+    def in_order(shift, compute, ahead=4):
+        order = [HOME] + [i for i in range(len(SHIFTS)) if i != HOME]
+        for place in range(len(order) + ahead):
+            if place < len(order):
+                shift(order[place])
+            if place >= ahead:
+                compute(order[place - ahead])
+
+    def apply(source, target, last, masked=False):
         tiles = range(3) if source is None else range(2)
 
         def shift(i):
@@ -221,6 +235,19 @@
                     ref = ext.at[k] if source is None else chain.at[source, k]
                     for t, value in enumerate(shifted([ref[t, rows, :] for t in tiles], i)):
                         sh[i, t, k, rows, :] = value
+                    if masked:
+                        for t, value in enumerate(shifted([words[k, t, rows, :] for t in tiles], i)):
+                            sword[i, t, k, rows, :] = value
+
+        def present(i, dx, t, rt):
+            d = (dx, *SHIFTS[i])
+            if d > (0, 0, 0):
+                c, m = FLAGS[d]
+                word = sword[HOME, t, c, pl.ds(2 + 4 * rt, 8), :]
+            else:
+                c, m = FLAGS[tuple(-v for v in d)]
+                word = sword[i, t, c, pl.ds(2 + 4 * rt + dx, 8), :]
+            return (word & (1 << m)) != 0
 
         sides = [(t, rt) for t in range(2) for rt in range(1 if last else 2)]
         acc = {side: [None] * 3 for side in sides}
@@ -232,18 +259,19 @@
                     v = [sh[i, t, k, pl.ds(dx + 2 + 4 * rt, 8), :] for k in range(3)]
                     u = [coef[t, rt, n, k] for k in range(3)]
                     iso = coef[t, rt, n, 3]
+                    if masked:
+                        there = present(i, dx, t, rt)
+                        u = [jnp.where(there, value, 0.0) for value in u]
+                        iso = jnp.where(there, iso, 0.0)
+                        for k, value in enumerate((*u, iso)):
+                            coef[t, rt, n, k] = value
                     dot = u[0] * v[0] + u[1] * v[1] + u[2] * v[2]
                     for k in range(3):
                         term = u[k] * dot - iso * v[k]
                         old = acc[t, rt][k]
                         acc[t, rt][k] = term if old is None else old + term
 
-        ahead = 4
-        for i in range(len(SHIFTS) + ahead):
-            if i < len(SHIFTS):
-                shift(i)
-            if i >= ahead:
-                compute(i - ahead)
+        in_order(shift, compute)
         for t, rt in sides:
             scale = polo[t, pl.ds(2 + 4 * rt, 8), :]
             for k in range(3):
@@ -264,8 +292,9 @@
         out = jnp.where(zone[0][0], parts[0], jnp.where(zone[0][1], parts[1], parts[2]))
         return jnp.where(packed, out, 0.0)
 
-    pl.semaphore_wait(barrier, len(others))
+    pl.semaphore_wait(barrier, len(greeted))
     halo_start(0, send0.at[:, real], lambda b: recv0.at[b, :, real])
+    halo_start(3, sendf.at[:, real], lambda b: recvf.at[b, :, real])
     chain[...] = jnp.zeros_like(chain)
     halo_all(0).wait_recv()
 
@@ -274,23 +303,6 @@
         assemble(lambda b: recv0[b, 1], k, ext.at[k])
     assemble(lambda b: recv0[b, 2], 0, geo.at[4], 1.0)
     geo[3] = lax.rsqrt(geo[4])
-    flagged = [
-        jnp.where(zone[0][0], 0.0, recv0[b, 2]) * float(2 ** FLAG_TILES) for b in range(18)
-    ]
-    for n in range(FLAG_TILES):
-        for b in range(18):
-            flagged[b] = flagged[b] + recv0[b, 3 + n] * float(2 ** n)
-    for k in range(3):
-        assemble(lambda b: flagged[b], k, words.at[k])
-
-    for i in range(len(SHIFTS)):
-        for rows in halves:
-            for k in range(4):
-                for t, value in enumerate(shifted([geo[k, t, rows, :] for t in range(3)], i)):
-                    sgeo[i, t, k, rows, :] = value
-            for k in range(3):
-                for t, value in enumerate(shifted([words[k, t, rows, :] for t in range(3)], i)):
-                    sword[i, t, k, rows, :] = value.astype(jnp.int32)
     for half in range(2):
         rows = pl.ds(8 * half, 8)
         r = [roll(geo[4, t, rows, :], -ORIGIN) for t in range(3)]
@@ -298,40 +310,49 @@
             polo[t, rows, :] = jnp.where(lane < LANES - ORIGIN, r[t], r[t + 1])
 
     def geometry(t, carry):
-        for rt in range(2):
-            base = 2 + 4 * rt
-            here = [sgeo[HOME, t, k, pl.ds(base, 8), :] for k in range(4)]
-            flags = [sword[HOME, t, k, pl.ds(base, 8), :] for k in range(3)]
-            damped = here[3] * thole_damping
-            for i, s in enumerate(SHIFTS):
+        def shift(i):
+            a = ORIGIN + SHIFTS[i][0] * WIDE + SHIFTS[i][1]
+            for rows in halves:
+                for k in range(4):
+                    pair = [roll(geo[k, t + u, rows, :], -a) for u in range(2)]
+                    sgeo[i, t, k, rows, :] = jnp.where(lane < LANES - a, pair[0], pair[1])
+
+        def compute(i):
+            for rt in range(2):
+                base = 2 + 4 * rt
                 for j, dx in enumerate(SPAN[i]):
                     n = FIRST[i] + j
-                    d = (dx, *s)
+                    d = (dx, *SHIFTS[i])
                     rows = pl.ds(base + dx, 8)
-                    if d > (0, 0, 0):
-                        c, m = FLAGS[d]
-                        word = flags[c]
-                    else:
-                        c, m = FLAGS[tuple(-v for v in d)]
-                        word = sword[i, t, c, rows, :]
-                    present = (word & (1 << m)) != 0
-                    sep = [sgeo[i, t, k, rows, :] - here[k] for k in range(3)]
+                    sep = [sgeo[i, t, k, rows, :] - sgeo[HOME, t, k, pl.ds(base, 8), :] for k in range(3)]
                     sep = [v + e * site_spacing if e else v for v, e in zip(sep, d)]
                     sq = sep[0] * sep[0] + sep[1] * sep[1] + sep[2] * sep[2]
                     inv = lax.rsqrt(sq)
-                    damp = (damped * sgeo[i, t, 3, rows, :]) * (sq * (sq * inv))
+                    roots = sgeo[HOME, t, 3, pl.ds(base, 8), :] * sgeo[i, t, 3, rows, :]
+                    damp = (thole_damping * roots) * (sq * (sq * inv))
                     fall = jnp.exp(-damp)
                     inv2 = inv * inv
                     inv3 = inv2 * inv
-                    iso = jnp.where(present, (1.0 - fall) * inv3, 0.0)
                     rad = (1.0 - (1.0 + damp) * fall) * (3.0 * inv3 * inv2)
-                    root = jnp.where(present, rad * lax.rsqrt(rad), 0.0)
+                    root = rad * lax.rsqrt(rad)
                     for k in range(3):
                         coef[t, rt, n, k] = root * sep[k]
-                    coef[t, rt, n, 3] = iso
+                    coef[t, rt, n, 3] = (1.0 - fall) * inv3
+
+        in_order(shift, compute)
         return carry
 
     lax.fori_loop(0, 2, geometry, 0)
+
+    halo_all(3).wait_recv()
+    flagged = []
+    for b in range(18):
+        total = jnp.where(zone[0][0], 0.0, recv0[b, 2]) * float(2 ** FLAG_TILES)
+        for n in range(FLAG_TILES):
+            total = total + recvf[b, n] * float(2 ** n)
+        flagged.append(total.astype(jnp.int32))
+    for k in range(3):
+        assemble(lambda b: flagged[b], k, words.at[k], 0)
 
     def dots_start(index, vectors, number):
         line = jnp.zeros((1, LANES), f32)
@@ -411,10 +432,10 @@
             for m in range(vectors)
         ])
 
-    def chain_of_three():
+    def chain_of_three(first=False):
         out = []
         for k in range(3):
-            apply(None if k == 0 else k - 1, k, k == 2)
+            apply(None if k == 0 else k - 1, k, k == 2, first and k == 0)
             out.append(pack(k))
         return out
 
@@ -428,7 +449,7 @@
         for k in range(3):
             assemble(lambda b: recv1[index, b], k, ext.at[k])
 
-    table[0] += chain_of_three()
+    table[0] += chain_of_three(True)
     share(0, table[0][2])
     dots_start(0, table[0], 4)
     receive(0)
@@ -460,8 +481,9 @@
     out_ref[1] = residual
     out_ref[2, 0:1, :] = line
 
+    for index in range(4):
+        halo_all(index).wait_send()
     for index in range(3):
-        halo_all(index).wait_send()
         dots_all(index).wait_send()
 
 
@@ -499,7 +521,7 @@
                 pltpu.VMEM((3, *wide), f32),
                 pltpu.VMEM((shifts, 2, 3, 16, LANES), f32),
                 pltpu.VMEM((5, *wide), f32),
-                pltpu.VMEM((3, *wide), f32),
+                pltpu.VMEM((3, *wide), jnp.int32),
                 pltpu.VMEM((shifts, 2, 4, 16, LANES), f32),
                 pltpu.VMEM((shifts, 2, 3, 16, LANES), jnp.int32),
                 pltpu.VMEM(near, f32),
@@ -507,12 +529,14 @@
                 pltpu.VMEM((3, 3, *near), f32),
                 pltpu.VMEM((TILES, ROWS, LANES), f32),
                 pltpu.VMEM((18, TILES, ROWS, LANES), f32),
+                pltpu.VMEM((FLAG_TILES, ROWS, LANES), f32),
+                pltpu.VMEM((18, FLAG_TILES, ROWS, LANES), f32),
                 pltpu.VMEM((2, ROWS, LANES), f32),
                 pltpu.VMEM((2, 18, ROWS, LANES), f32),
                 pltpu.VMEM((3, 1, LANES), f32),
                 pltpu.VMEM((3, count, 1, LANES), f32),
-                pltpu.SemaphoreType.DMA((3,)),
-                pltpu.SemaphoreType.DMA((3,)),
+                pltpu.SemaphoreType.DMA((4,)),
+                pltpu.SemaphoreType.DMA((4,)),
                 pltpu.SemaphoreType.DMA((3,)),
                 pltpu.SemaphoreType.DMA((3,)),
                 pltpu.SemaphoreType.DMA((4,)),

time: 48.5 us -> 44.9 us (0.926)
  Pallas kernels: 47.7 us -> 44.1 us
    pallas_call x1, Pallas kernels: 47 us -> 43.4 us  [local(): pl.pallas_call(functools.partial(kernel, sizes), out_shape=pltpu.VMEM((3,...]
where the time goes in v4:
time: 44.9 us; the launch traced here: 44.8 us
  Pallas kernels  44.1 us (98%)
  between operations  0.64 us (1%)
    pallas_call x1, Pallas kernels, local(): pl.pallas_call(functools.partial(kernel, sizes), out_shape=pltpu.VMEM((3,...  43.4 us

profile of v4, /device:TPU:1, one launch (start us, length us, event | category | flops | bytes accessed | tf_op | source)
XLA Modules:
  0.0 44.8 jit_solution(10118581533376792986)
XLA Ops:
  0.6 43.4 %shard_map.67.in_ref = f32[3,8,128]{2,1,0:T(8,128)S(1)} custom-call(f32[6,6,3,6]{3,2,1,0:T(4,128)} %bitcast.5, f32[6,6,6]{2,1,0:T(8,128)} %pol_in.1, f32[6,6,3,6]{3,2,1,0:T(4,128)} %bitcast.6, s32[6,6,6,56]{3,2,1,0:T(8,128)} %nb_in.1), custom_call_target="tpu_custom_call" | custom-call | tf_op jit(solution)/shard_map/pallas_call | solution.py:511
  44.0 0.8 %shard_map.68 = (f32[6,6,3,6]{3,2,1,0:T(4,128)}, f32[6,6,3,6]{3,2,1,0:T(4,128)}, f32[1,8]{1,0:T(1,128)}) custom-call(f32[3,8,128]{2,1,0:T(8,128)S(1)} %shard_map.67.in_ref), custom_call_target="tpu_custom_call" | custom-call | tf_op jit(solution)/shard_map/pallas_call | solution.py:551

commit v5 on v4

--- a/solution.py
+++ b/solution.py
@@ -77,7 +77,13 @@
     others = [
         (a, b, c) for a in range(nx) for b in range(ny) for c in range(nz) if (a, b, c) != (0, 0, 0)
     ]
-    others.sort(key=lambda o: -(min(o[0], nx - o[0]) + 2 * min(o[1], ny - o[1]) + 2 * min(o[2], nz - o[2])))
+
+    def hops(o):
+        ring = lambda v: min(v % 4, -v % 4)
+        along = max(ring(o[2] // 4), ring(o[2] // 4 + 1)) if o[2] % 4 else ring(o[2] // 4)
+        return 4 * (ring(o[1]) + ring(o[2] % 4) + along) + o[0]
+
+    others.sort(key=lambda o: -hops(o))
 
     barrier = pltpu.get_barrier_semaphore()
     loads = [
@@ -162,11 +168,11 @@
 
     real = pl.ds(0, EDGE)
 
-    def halo_start(index, src, get_dst):
+    def halo_start(index, src, get_dst, wanted=lambda o: True):
         for oy in (-1, 1, 0):
             for oz in (-1, 1, 0):
                 for ox in (1, 0):
-                    if (ox, oy, oz) == (0, 0, 0):
+                    if (ox, oy, oz) == (0, 0, 0) or not wanted((ox, oy, oz)):
                         continue
                     back = ox * 9 + (1 - oy) * 3 + 1 - oz
                     pltpu.make_async_remote_copy(
@@ -178,7 +184,8 @@
     def halo_all(index):
         some = pl.ds(0, 17)
         ref = {
-            0: recv0.at[some, :, real], 3: recvf.at[some, :, real],
+            0: recv0.at[some, :, real],
+            3: recvf.at[pl.ds(0, 9), :, real], 4: recvf.at[pl.ds(0, 8), :, real],
             1: recv1.at[0, some, real], 2: recv1.at[1, some, real],
         }[index]
         return pltpu.make_async_remote_copy(
@@ -228,6 +235,10 @@
 
     def apply(source, target, last, masked=False):
         tiles = range(3) if source is None else range(2)
+        needed = [
+            {FLAGS[tuple(-v for v in (dx, *s))][0] for dx in span if (dx, *s) < (0, 0, 0)} for s, span in zip(SHIFTS, SPAN)
+        ]
+        needed[HOME] = {0, 1, 2}
 
         def shift(i):
             for k in range(3):
@@ -235,7 +246,7 @@
                     ref = ext.at[k] if source is None else chain.at[source, k]
                     for t, value in enumerate(shifted([ref[t, rows, :] for t in tiles], i)):
                         sh[i, t, k, rows, :] = value
-                    if masked:
+                    if masked and k in needed[i]:
                         for t, value in enumerate(shifted([words[k, t, rows, :] for t in tiles], i)):
                             sword[i, t, k, rows, :] = value
 
@@ -294,7 +305,7 @@
 
     pl.semaphore_wait(barrier, len(greeted))
     halo_start(0, send0.at[:, real], lambda b: recv0.at[b, :, real])
-    halo_start(3, sendf.at[:, real], lambda b: recvf.at[b, :, real])
+    halo_start(3, sendf.at[:, real], lambda b: recvf.at[b, :, real], lambda o: o[0] == 0 or o == (1, 0, 0))
     chain[...] = jnp.zeros_like(chain)
     halo_all(0).wait_recv()
 
@@ -345,8 +356,17 @@
     lax.fori_loop(0, 2, geometry, 0)
 
     halo_all(3).wait_recv()
+    for b in range(9):
+        if b != own:
+            pltpu.make_async_remote_copy(
+                src_ref=recvf.at[b, :, real], dst_ref=recvf.at[9 + b, :, real],
+                send_sem=halo_send.at[4], recv_sem=halo_recv.at[4],
+                device_id=at(1, 0, 0), device_id_type=MESH,
+            ).start()
     flagged = []
     for b in range(18):
+        if b == 9:
+            halo_all(4).wait_recv()
         total = jnp.where(zone[0][0], 0.0, recv0[b, 2]) * float(2 ** FLAG_TILES)
         for n in range(FLAG_TILES):
             total = total + recvf[b, n] * float(2 ** n)
@@ -432,12 +452,12 @@
             for m in range(vectors)
         ])
 
-    def chain_of_three(first=False):
-        out = []
+    def chain_of_three(powers, first=False, between=None):
         for k in range(3):
+            if k == 2 and between is not None:
+                between()
             apply(None if k == 0 else k - 1, k, k == 2, first and k == 0)
-            out.append(pack(k))
-        return out
+            powers.append(pack(k))
 
     def share(index, value):
         send1[index] = value
@@ -449,19 +469,23 @@
         for k in range(3):
             assemble(lambda b: recv1[index, b], k, ext.at[k])
 
-    table[0] += chain_of_three(True)
+    def after_first():
+        known.extend(scalars(dots_finish(0, 4), known, 2))
+
+    def after_second():
+        known.extend(scalars(dots_finish(1, 6), known, 3))
+
+    chain_of_three(table[0], first=True)
     share(0, table[0][2])
     dots_start(0, table[0], 4)
     receive(0)
-    table[0] += chain_of_three()
-    known += scalars(dots_finish(0, 4), known, 2)
+    chain_of_three(table[0], between=after_first)
     lanczos(5)
     lanczos(4)
     share(1, table[2][3])
     dots_start(1, table[2], 6)
     receive(1)
-    table[2] += chain_of_three()
-    known += scalars(dots_finish(1, 6), known, 3)
+    chain_of_three(table[2], between=after_second)
     table[1].append(table[2][4] * known[1][4] + known[1][2] * table[1][4] + known[1][3] * table[0][4])
     for vectors in (6, 5, 4):
         lanczos(vectors)
@@ -481,7 +505,7 @@
     out_ref[1] = residual
     out_ref[2, 0:1, :] = line
 
-    for index in range(4):
+    for index in range(5):
         halo_all(index).wait_send()
     for index in range(3):
         dots_all(index).wait_send()
@@ -535,8 +559,8 @@
                 pltpu.VMEM((2, 18, ROWS, LANES), f32),
                 pltpu.VMEM((3, 1, LANES), f32),
                 pltpu.VMEM((3, count, 1, LANES), f32),
-                pltpu.SemaphoreType.DMA((4,)),
-                pltpu.SemaphoreType.DMA((4,)),
+                pltpu.SemaphoreType.DMA((5,)),
+                pltpu.SemaphoreType.DMA((5,)),
                 pltpu.SemaphoreType.DMA((3,)),
                 pltpu.SemaphoreType.DMA((3,)),
                 pltpu.SemaphoreType.DMA((4,)),

time: 44.9 us -> 44.2 us (0.984)
  Pallas kernels: 44.1 us -> 43.4 us
    pallas_call x1, Pallas kernels: 43.4 us -> 42.6 us  [local(): pl.pallas_call(functools.partial(kernel, sizes), out_shape=pltpu.VMEM((3,...]
where the time goes in v5:
time: 44.2 us; the launch traced here: 44 us
  Pallas kernels  43.4 us (98%)
  between operations  0.64 us (1%)
    pallas_call x1, Pallas kernels, local(): pl.pallas_call(functools.partial(kernel, sizes), out_shape=pltpu.VMEM((3,...  42.6 us

profile of v5, /device:TPU:1, one launch (start us, length us, event | category | flops | bytes accessed | tf_op | source)
XLA Modules:
  0.0 44.0 jit_solution(16493982825214589943)
XLA Ops:
  0.6 42.6 %shard_map.67.in_ref = f32[3,8,128]{2,1,0:T(8,128)S(1)} custom-call(f32[6,6,3,6]{3,2,1,0:T(4,128)} %bitcast.5, f32[6,6,6]{2,1,0:T(8,128)} %pol_in.1, f32[6,6,3,6]{3,2,1,0:T(4,128)} %bitcast.6, s32[6,6,6,56]{3,2,1,0:T(8,128)} %nb_in.1), custom_call_target="tpu_custom_call" | custom-call | tf_op jit(solution)/shard_map/pallas_call | solution.py:535
  43.3 0.8 %shard_map.68 = (f32[6,6,3,6]{3,2,1,0:T(4,128)}, f32[6,6,3,6]{3,2,1,0:T(4,128)}, f32[1,8]{1,0:T(1,128)}) custom-call(f32[3,8,128]{2,1,0:T(8,128)S(1)} %shard_map.67.in_ref), custom_call_target="tpu_custom_call" | custom-call | tf_op jit(solution)/shard_map/pallas_call | solution.py:575

commit v6 on v5

--- a/solution.py
+++ b/solution.py
@@ -158,8 +158,8 @@
         return out.astype(f32)
 
     send0[0] = jit
-    send0[1] = x
-    send0[2] = pol0 + flag_tile(FLAG_TILES)
+    send0[1] = pol0 + flag_tile(FLAG_TILES)
+    send0[2] = x
     for n in range(FLAG_TILES):
         sendf[n] = flag_tile(n)
     own = 4
@@ -184,7 +184,7 @@
     def halo_all(index):
         some = pl.ds(0, 17)
         ref = {
-            0: recv0.at[some, :, real],
+            0: recv0.at[some, pl.ds(0, 2), real], 5: recv0.at[some, pl.ds(2, 1), real],
             3: recvf.at[pl.ds(0, 9), :, real], 4: recvf.at[pl.ds(0, 8), :, real],
             1: recv1.at[0, some, real], 2: recv1.at[1, some, real],
         }[index]
@@ -304,15 +304,16 @@
         return jnp.where(packed, out, 0.0)
 
     pl.semaphore_wait(barrier, len(greeted))
-    halo_start(0, send0.at[:, real], lambda b: recv0.at[b, :, real])
+    early, late = pl.ds(0, 2), pl.ds(2, 1)
+    halo_start(0, send0.at[early, real], lambda b: recv0.at[b, early, real])
     halo_start(3, sendf.at[:, real], lambda b: recvf.at[b, :, real], lambda o: o[0] == 0 or o == (1, 0, 0))
+    halo_start(5, send0.at[late, real], lambda b: recv0.at[b, late, real])
     chain[...] = jnp.zeros_like(chain)
     halo_all(0).wait_recv()
 
     for k in range(3):
         assemble(lambda b: recv0[b, 0], k, geo.at[k])
-        assemble(lambda b: recv0[b, 1], k, ext.at[k])
-    assemble(lambda b: recv0[b, 2], 0, geo.at[4], 1.0)
+    assemble(lambda b: recv0[b, 1], 0, geo.at[4], 1.0)
     geo[3] = lax.rsqrt(geo[4])
     for half in range(2):
         rows = pl.ds(8 * half, 8)
@@ -367,12 +368,15 @@
     for b in range(18):
         if b == 9:
             halo_all(4).wait_recv()
-        total = jnp.where(zone[0][0], 0.0, recv0[b, 2]) * float(2 ** FLAG_TILES)
+        total = jnp.where(zone[0][0], 0.0, recv0[b, 1]) * float(2 ** FLAG_TILES)
         for n in range(FLAG_TILES):
             total = total + recvf[b, n] * float(2 ** n)
         flagged.append(total.astype(jnp.int32))
     for k in range(3):
         assemble(lambda b: flagged[b], k, words.at[k], 0)
+    halo_all(5).wait_recv()
+    for k in range(3):
+        assemble(lambda b: recv0[b, 2], k, ext.at[k])
 
     def dots_start(index, vectors, number):
         line = jnp.zeros((1, LANES), f32)
@@ -505,7 +509,7 @@
     out_ref[1] = residual
     out_ref[2, 0:1, :] = line
 
-    for index in range(5):
+    for index in range(6):
         halo_all(index).wait_send()
     for index in range(3):
         dots_all(index).wait_send()
@@ -559,8 +563,8 @@
                 pltpu.VMEM((2, 18, ROWS, LANES), f32),
                 pltpu.VMEM((3, 1, LANES), f32),
                 pltpu.VMEM((3, count, 1, LANES), f32),
-                pltpu.SemaphoreType.DMA((5,)),
-                pltpu.SemaphoreType.DMA((5,)),
+                pltpu.SemaphoreType.DMA((6,)),
+                pltpu.SemaphoreType.DMA((6,)),
                 pltpu.SemaphoreType.DMA((3,)),
                 pltpu.SemaphoreType.DMA((3,)),
                 pltpu.SemaphoreType.DMA((4,)),

time: 44.2 us -> 44.6 us (level)
  no operation moved by 1% of the time
where the time goes in v6:
time: 44.6 us; the launch traced here: 44.4 us
  Pallas kernels  43.8 us (98%)
  between operations  0.64 us (1%)
    pallas_call x1, Pallas kernels, local(): pl.pallas_call(functools.partial(kernel, sizes), out_shape=pltpu.VMEM((3,...  43 us

profile of v6, /device:TPU:1, one launch (start us, length us, event | category | flops | bytes accessed | tf_op | source)
XLA Modules:
  0.0 44.4 jit_solution(2219454093387983761)
XLA Ops:
  0.6 43.0 %shard_map.67.in_ref = f32[3,8,128]{2,1,0:T(8,128)S(1)} custom-call(f32[6,6,3,6]{3,2,1,0:T(4,128)} %bitcast.5, f32[6,6,6]{2,1,0:T(8,128)} %pol_in.1, f32[6,6,3,6]{3,2,1,0:T(4,128)} %bitcast.6, s32[6,6,6,56]{3,2,1,0:T(8,128)} %nb_in.1), custom_call_target="tpu_custom_call" | custom-call | tf_op jit(solution)/shard_map/pallas_call | solution.py:539
  43.7 0.8 %shard_map.68 = (f32[6,6,3,6]{3,2,1,0:T(4,128)}, f32[6,6,3,6]{3,2,1,0:T(4,128)}, f32[1,8]{1,0:T(1,128)}) custom-call(f32[3,8,128]{2,1,0:T(8,128)S(1)} %shard_map.67.in_ref), custom_call_target="tpu_custom_call" | custom-call | tf_op jit(solution)/shard_map/pallas_call | solution.py:579

commit v7 on v5

--- a/solution.py
+++ b/solution.py
@@ -94,7 +94,7 @@
     ]
     for load in loads:
         load.start()
-    greeted = [o for o in others if o[1] in GREET_Y and o[2] in GREET_Z]
+    greeted = [o for o in others if o[2] in GREET_Z and (o[1] in GREET_Y[1:] or o[1] == 0 and o[2] in GREET_Z[::6] + (1,))]
     for o in greeted:
         pl.semaphore_signal(barrier, inc=1, device_id=at(*o), device_id_type=MESH)
     lane = lax.broadcasted_iota(jnp.int32, (ROWS, LANES), 1)

time: 44.2 us -> 44.1 us (level)
  no operation moved by 1% of the time
where the time goes in v7:
time: 44.1 us; the launch traced here: 44 us
  Pallas kernels  43.4 us (98%)
  between operations  0.64 us (1%)
    pallas_call x1, Pallas kernels, local(): pl.pallas_call(functools.partial(kernel, sizes), out_shape=pltpu.VMEM((3,...  42.6 us

profile of v7, /device:TPU:1, one launch (start us, length us, event | category | flops | bytes accessed | tf_op | source)
XLA Modules:
  0.0 44.0 jit_solution(6714761488120877645)
XLA Ops:
  0.6 42.6 %shard_map.67.in_ref = f32[3,8,128]{2,1,0:T(8,128)S(1)} custom-call(f32[6,6,3,6]{3,2,1,0:T(4,128)} %bitcast.5, f32[6,6,6]{2,1,0:T(8,128)} %pol_in.1, f32[6,6,3,6]{3,2,1,0:T(4,128)} %bitcast.6, s32[6,6,6,56]{3,2,1,0:T(8,128)} %nb_in.1), custom_call_target="tpu_custom_call" | custom-call | tf_op jit(solution)/shard_map/pallas_call | solution.py:535
  43.2 0.8 %shard_map.68 = (f32[6,6,3,6]{3,2,1,0:T(4,128)}, f32[6,6,3,6]{3,2,1,0:T(4,128)}, f32[1,8]{1,0:T(1,128)}) custom-call(f32[3,8,128]{2,1,0:T(8,128)S(1)} %shard_map.67.in_ref), custom_call_target="tpu_custom_call" | custom-call | tf_op jit(solution)/shard_map/pallas_call | solution.py:575
